TPU v7x, 32 devices: a whole 2x2x4 slice. The times are simulated.
32 devices in a mesh: batch: 8 (over y, x, core), seq: 4 (over z).
Axes of the slice: x: 2, y: 2, z: 4, core: 2. Of those that a mesh axis runs over, the one named last changes fastest.
Arguments:
- tokens: bfloat16 [32768, 1024], P(('batch', 'seq')), may hold values from -6 to 6
- seq_lengths: int32 [8, 4], P('batch'), may hold values from 0 to 2048, as said below
- attn_gain: float32 [1024], replicated, may hold values from 0.5 to 1.5
- attn_shift: float32 [1024], replicated, may hold values from -2 to 2
- qkv_weight: bfloat16 [1024, 3072], replicated, may hold values from -0.1875 to 0.1875
- qkv_bias: float32 [3072], replicated, may hold values from -3 to 3
- dense_weight: bfloat16 [1024, 1024], replicated, may hold values from -1.5 to 1.5
- dense_bias: float32 [1024], replicated, may hold values from -2 to 2
- mlp_gain: float32 [1024], replicated, may hold values from 0.5 to 1.5
- mlp_shift: float32 [1024], replicated, may hold values from -2 to 2
- expand_weight: bfloat16 [1024, 4096], replicated, may hold values from -0.1875 to 0.1875
- expand_bias: float32 [4096], replicated, may hold values from -3 to 3
- reduce_weight: bfloat16 [4096, 1024], replicated, may hold values from -0.09375 to 0.09375
- reduce_bias: float32 [1024], replicated, may hold values from -2 to 2
- out_grad: bfloat16 [32768, 1024], P(('batch', 'seq')), may hold values from -6 to 6
Outputs:
- layer_out: bfloat16 [32768, 1024], P(('batch', 'seq'))
- input_grad: bfloat16 [32768, 1024], P(('batch', 'seq'))
- attngain_grad: float32 [1024], P(('batch', 'seq'))
- attnshift_grad: float32 [1024], P(('batch', 'seq'))
- qkvweight_grad: float32 [1024, 3072], P(('batch', 'seq'))
- qkvbias_grad: float32 [3072], P(('batch', 'seq'))
- denseweight_grad: float32 [1024, 1024], P(('batch', 'seq'))
- densebias_grad: float32 [1024], P(('batch', 'seq'))
- mlpgain_grad: float32 [1024], P(('batch', 'seq'))
- mlpshift_grad: float32 [1024], P(('batch', 'seq'))
- expandweight_grad: float32 [1024, 4096], P(('batch', 'seq'))
- expandbias_grad: float32 [4096], P(('batch', 'seq'))
- reduceweight_grad: float32 [4096, 1024], P(('batch', 'seq'))
- reducebias_grad: float32 [1024], P(('batch', 'seq'))
Inputs may be any that keep to these rules, and one draw needn't show every extreme that they name: `seq_lengths`: row b lists the lengths of the two or three sequences of batch group b in the order in which they lie among its 4096 tokens: each is 1024 or 2048, they add up to 4096, and the unused entries, at the end of the row, are 0. Every group holds a sequence of 2048 tokens.
All inputs are finite; a program needn't handle non-finite values.
Results may differ from a plain program's by a relative error of at most 0.0093.
Values may be sent and summed in bfloat16 or wider, within the bound.
A program may use at most 192 MiB of HBM per device.

v0:
```python
from functools import partial
import math

import jax
import jax.numpy as jnp
from jax import lax
from jax.experimental import pallas as pl
from jax.experimental.pallas import tpu as pltpu
from jax.sharding import PartitionSpec as P


HEAD_DIM = 64
ROT = 16
PAIR = 2 * HEAD_DIM
EPSILON = 1e-05
MASKED = -1e30
SCALE = 1.0 / math.sqrt(HEAD_DIM)
QB = 256
FB = 1024
STEP_PAIRS = 2
ROWS = 128
F32 = jnp.float32
BF16 = jnp.bfloat16
VMEM_LIMIT = 60 << 20


def dot(left, right):
    return jnp.dot(left, right, preferred_element_type=F32)


def dot_t(left, right):
    return lax.dot_general(left, right, (((1,), (1,)), ((), ())), preferred_element_type=F32)


def params():
    return pltpu.CompilerParams(vmem_limit_bytes=VMEM_LIMIT)


def cost(flops, nbytes):
    return pl.CostEstimate(flops=int(flops), bytes_accessed=int(nbytes), transcendentals=0)


def whole(shape):
    return pl.BlockSpec(shape, lambda i: (0,) * len(shape), pipeline_mode=pl.Buffered(1))


def statistics(x):
    mean = jnp.mean(x, axis=-1, keepdims=True)
    centered = x - mean
    variance = jnp.mean(centered * centered, axis=-1, keepdims=True)
    rstd = lax.rsqrt(variance + EPSILON)
    return centered * rstd, rstd


def norm_rows(x_ref, gain_ref, shift_ref, out_ref):
    def step(i, carry):
        rows = pl.ds(pl.multiple_of(i * ROWS, ROWS), ROWS)
        xn, _ = statistics(x_ref[rows, :].astype(F32))
        out_ref[rows, :] = (xn * gain_ref[...] + shift_ref[...]).astype(BF16)
        return carry

    lax.fori_loop(0, x_ref.shape[0] // ROWS, step, 0)


def norm_back(x_ref, gain_ref, grad_ref, gaingrad_ref, shiftgrad_ref, emit):
    gaingrad_ref[...] = jnp.zeros_like(gaingrad_ref)
    shiftgrad_ref[...] = jnp.zeros_like(shiftgrad_ref)

    def step(i, carry):
        rows = pl.ds(pl.multiple_of(i * ROWS, ROWS), ROWS)
        xn, rstd = statistics(x_ref[rows, :].astype(F32))
        grad = grad_ref[rows, :]
        gaingrad_ref[...] += jnp.sum(grad * xn, axis=0, keepdims=True)
        shiftgrad_ref[...] += jnp.sum(grad, axis=0, keepdims=True)
        scaled = grad * gain_ref[...]
        mean_s = jnp.mean(scaled, axis=-1, keepdims=True)
        mean_sx = jnp.mean(scaled * xn, axis=-1, keepdims=True)
        emit(rows, rstd * (scaled - mean_s - xn * mean_sx))
        return carry

    lax.fori_loop(0, x_ref.shape[0] // ROWS, step, 0)


def build_tables(angle_ref, tab_ref):
    half = ROT // 2
    cos8, sin8 = angle_ref[0:half, :], angle_ref[half:ROT, :]
    rest = HEAD_DIM - ROT
    count = cos8.shape[1]
    ones = jnp.ones((rest, count), F32)
    zeros = jnp.zeros((rest, count), F32)
    z8 = jnp.zeros_like(sin8)
    tab_ref[0] = jnp.concatenate([cos8, cos8, ones] * 2, axis=0).T
    tab_ref[1] = jnp.concatenate([-sin8, z8, zeros] * 2, axis=0).T
    tab_ref[2] = jnp.concatenate([z8, sin8, zeros] * 2, axis=0).T


def turn(u, tab_ref, sign):
    half = ROT // 2
    ahead = pltpu.roll(u, PAIR - half, 1)
    behind = pltpu.roll(u, half, 1)
    return u * tab_ref[0] + sign * (ahead * tab_ref[1] + behind * tab_ref[2])


def low_lanes(shape):
    return lax.broadcasted_iota(jnp.int32, shape, 1) < HEAD_DIM


def project_kernel(x_ref, gain_ref, shift_ref, w_ref, b_ref, ang_ref, og_ref, wd_ref,
                   q_ref, kv_ref, do_ref, norm, tab):
    @pl.when(pl.program_id(0) == 0)
    def _():
        norm_rows(x_ref, gain_ref, shift_ref, norm)
        build_tables(ang_ref, tab)

    for n in range(STEP_PAIRS):
        cols = slice(n * 3 * PAIR, (n + 1) * 3 * PAIR)
        mine = slice(n * PAIR, (n + 1) * PAIR)
        mixed = dot(norm[...], w_ref[:, cols]) + b_ref[:, cols]
        t0, t1, t2 = mixed[:, :PAIR], mixed[:, PAIR:2 * PAIR], mixed[:, 2 * PAIR:]
        low = low_lanes(t0.shape)
        q = jnp.where(low, t0, t1)
        k = pltpu.roll(jnp.where(low, t2, t0), HEAD_DIM, 1)
        v = jnp.where(low, t1, t2)
        q_ref[:, mine] = turn(q, tab, 1.0).astype(BF16)
        kv_ref[0, :, mine] = turn(k, tab, 1.0).astype(BF16)
        kv_ref[1, :, mine] = v.astype(BF16)
    do_ref[...] = dot_t(og_ref[...], wd_ref[...]).astype(BF16)


def project(x, gain, shift, w, b, ang, og, wd):
    rows, width = x.shape
    wide = STEP_PAIRS * PAIR
    tok = pl.BlockSpec((rows, wide), lambda i: (0, i))
    return pl.pallas_call(
        project_kernel,
        grid=(width // wide,),
        out_shape=(
            jax.ShapeDtypeStruct((rows, width), BF16),
            jax.ShapeDtypeStruct((2, rows, width), BF16),
            jax.ShapeDtypeStruct((rows, width), BF16),
        ),
        in_specs=[
            whole((rows, width)), whole((1, width)), whole((1, width)),
            pl.BlockSpec((width, 3 * wide), lambda i: (0, i)),
            pl.BlockSpec((1, 3 * wide), lambda i: (0, i)),
            whole(ang.shape), whole((rows, width)),
            pl.BlockSpec((wide, width), lambda i: (i, 0)),
        ],
        out_specs=(tok, pl.BlockSpec((2, rows, wide), lambda i: (0, 0, i)), tok),
        scratch_shapes=[pltpu.VMEM((rows, width), BF16), pltpu.VMEM((3, rows, PAIR), F32)],
        compiler_params=params(),
        cost_estimate=cost(8 * rows * width * width, 24 * rows * width),
        name="project",
    )(x, gain, shift, w, b, ang, og, wd)


def gelu_parts(h):
    z = jnp.abs(h) * math.sqrt(0.5)
    t = 1.0 / (1.0 + 0.5 * z)
    poly = jnp.full_like(t, 0.17087277)
    for c in (-0.82215223, 1.48851587, -1.13520398, 0.27886807, -0.18628806, 0.09678418,
              0.37409196, 1.00002368, -1.26551223):
        poly = poly * t + c
    zz = z * z
    tail = 0.5 * t * jnp.exp(poly - zz)
    cdf = jnp.where(h >= 0, 1.0 - tail, tail)
    slope = cdf + h * (jnp.exp(-zz) * (1.0 / math.sqrt(2.0 * math.pi)))
    return h * cdf, slope


def mlp_fwd_kernel(take, x_ref, gain_ref, shift_ref, we_ref, be_ref, wr_ref, og_ref,
                   mid_ref, slope_ref, dwr_ref, dog_ref, norm):
    step = pl.program_id(0)
    width = x_ref.shape[1]

    @pl.when(step == 0)
    def _():
        norm_rows(x_ref, gain_ref, shift_ref, norm)
        mid_ref[...] = jnp.zeros_like(mid_ref)
        dog_ref[...] = jnp.sum(og_ref[...].astype(F32), axis=0, keepdims=True)

    h = dot(norm[...], we_ref[...]) + be_ref[...]
    active, slope = gelu_parts(h)
    active = active.astype(BF16)
    slope_ref[...] = slope.astype(BF16)
    mid_ref[...] += dot(active, wr_ref[...])
    dwr = dot(active.T, og_ref[...]).astype(BF16)
    full = dwr_ref.shape[1] - GRAD_PAD
    ratio = full // width
    for piece in range(FB // take):
        group, j = piece // ratio, piece % ratio
        dwr_ref[group * take:(group + 1) * take, j * width:(j + 1) * width] = (
            dwr[piece * take:(piece + 1) * take, :])
    dwr_ref[:, full:] = jnp.zeros((dwr_ref.shape[0], GRAD_PAD), BF16)


def mlp_back_kernel(x_ref, gain_ref, shift_ref, we_ref, wr_ref, og_ref, slope_ref,
                    part_ref, dwe_ref, dbe_ref, dgain_ref, dshift_ref, norm, norm_t, sg):
    step = pl.program_id(0)

    @pl.when(step == 0)
    def _():
        norm_rows(x_ref, gain_ref, shift_ref, norm)
        norm_t[...] = norm[...].T
        sg[...] = jnp.zeros_like(sg)

    hidden = (dot_t(og_ref[...], wr_ref[...]) * slope_ref[...].astype(F32)).astype(BF16)
    dwe_ref[...] = dot(norm_t[...], hidden).astype(BF16)
    dbe_ref[...] = jnp.sum(hidden.astype(F32), axis=0, keepdims=True)
    sg[...] += dot_t(hidden, we_ref[...])

    @pl.when(step == pl.num_programs(0) - 1)
    def _():
        def emit(rows, part):
            part_ref[rows, :] = part

        norm_back(x_ref, gain_ref, sg, dgain_ref, dshift_ref, emit)


GRAD_PAD = 128


def mlp_specs(x):
    rows, width = x.shape
    full = whole((rows, width))
    vec = whole((1, width))
    up = pl.BlockSpec((width, FB), lambda i: (0, i))
    down = pl.BlockSpec((FB, width), lambda i: (i, 0))
    bias = pl.BlockSpec((1, FB), lambda i: (0, i))
    act = pl.BlockSpec((rows, FB), lambda i: (0, i))
    return full, vec, up, down, bias, act


def mlp_fwd(ndev, x, gain, shift, we, be, wr, og):
    rows, width = x.shape
    hidden = we.shape[1]
    full, vec, up, down, bias, act = mlp_specs(x)
    out_rows = hidden // (hidden // width)
    blk = FB * out_rows // hidden
    gshape = (out_rows, hidden + GRAD_PAD)
    return pl.pallas_call(
        partial(mlp_fwd_kernel, out_rows // ndev),
        grid=(hidden // FB,),
        out_shape=(jax.ShapeDtypeStruct((rows, width), F32), jax.ShapeDtypeStruct((rows, hidden), BF16),
                   jax.ShapeDtypeStruct(gshape, BF16), jax.ShapeDtypeStruct((1, width), F32)),
        in_specs=[full, vec, vec, up, bias, down, full],
        out_specs=(full, act, pl.BlockSpec((blk, gshape[1]), lambda i: (i, 0)), vec),
        scratch_shapes=[pltpu.VMEM((rows, width), BF16)],
        compiler_params=params(),
        cost_estimate=cost(6 * rows * width * hidden, 8 * width * hidden),
        name="mlp_fwd",
    )(x, gain, shift, we, be, wr, og)


def mlp_back(x, gain, shift, we, wr, og, slope):
    rows, width = x.shape
    hidden = we.shape[1]
    full, vec, up, down, bias, act = mlp_specs(x)
    vshape = jax.ShapeDtypeStruct((1, width), F32)
    return pl.pallas_call(
        mlp_back_kernel,
        grid=(hidden // FB,),
        out_shape=(jax.ShapeDtypeStruct((rows, width), F32),
                   jax.ShapeDtypeStruct((width, hidden + GRAD_PAD), BF16),
                   jax.ShapeDtypeStruct((1, hidden), F32), vshape, vshape),
        in_specs=[full, vec, vec, up, down, full, act],
        out_specs=(full, up, bias, vec, vec),
        scratch_shapes=[pltpu.VMEM((rows, width), BF16), pltpu.VMEM((width, rows), BF16),
                        pltpu.VMEM((rows, width), F32)],
        compiler_params=params(),
        cost_estimate=cost(6 * rows * width * hidden, 8 * width * hidden),
        name="mlp_back",
    )(x, gain, shift, we, wr, og, slope)


def attend_kernel(flag_ref, q_ref, kv_ref, kvp_ref, do_ref, o_ref, dq_ref, dkv_ref, dkvp_ref,
                  pt, ds, kvt, qm, dom):
    rows_all = q_ref.shape[0]
    nq = rows_all // QB

    def run(prev):
        base = 0 if prev else nq
        sources = [(kvp_ref, i) for i in range(nq)] + [(kv_ref, i) for i in range(nq)]

        def block(which, b):
            ref, i = sources[b]
            return ref[which, i * QB:(i + 1) * QB, :]

        for which in range(2):
            if prev:
                kvt[which, :, :rows_all] = kvp_ref[which].T
            kvt[which, :, rows_all:] = kv_ref[which].T
        lane = lax.broadcasted_iota(jnp.int32, (QB, PAIR), 1)
        sub = lax.broadcasted_iota(jnp.int32, (PAIR, QB), 0)
        causal = lax.broadcasted_iota(jnp.int32, (QB, QB), 0) <= lax.broadcasted_iota(
            jnp.int32, (QB, QB), 1)
        for j in range(nq):
            rows = slice(j * QB, (j + 1) * QB)
            q = q_ref[rows, :] * jnp.asarray(SCALE, BF16)
            qt = q.T
            dot_rows = do_ref[rows, :].astype(F32).T
            blocks = range(base, nq + j + 1)
            k0, k1 = base * QB, (nq + j + 1) * QB
            outs, scaled, dqs = [], [], []
            for h in range(2):
                hs = slice(h * HEAD_DIM, (h + 1) * HEAD_DIM)
                qm[h, rows, :] = jnp.where((lane < HEAD_DIM) == (h == 0), q, jnp.zeros_like(q))
                qtm = jnp.where((sub < HEAD_DIM) == (h == 0), qt, jnp.zeros_like(qt))
                scores, top = [], None
                for b in blocks:
                    s = dot(block(0, b), qtm)
                    if b == nq + j:
                        s = jnp.where(causal, s, MASKED)
                    scores.append(s)
                    part = jnp.max(s.reshape(QB // 8, 8, QB), axis=0)
                    top = part if top is None else jnp.maximum(top, part)
                top = jnp.max(top, axis=0, keepdims=True)
                total = None
                for b, s in zip(blocks, scores):
                    p = jnp.exp(s - top)
                    part = jnp.sum(p.reshape(QB // 8, 8, QB), axis=0)
                    total = part if total is None else total + part
                    pt[h, b * QB:(b + 1) * QB, rows] = p.astype(BF16)
                inv = 1.0 / jnp.sum(total, axis=0, keepdims=True)
                out_t = dot(kvt[1, hs, k0:k1], pt[h, k0:k1, rows]) * inv
                dol_t = dot_rows[hs] * inv
                delta = jnp.sum(dol_t * out_t, axis=0, keepdims=True)
                outs.append(out_t)
                scaled.append(dol_t)
                zero = jnp.zeros((HEAD_DIM, QB), BF16)
                dol_b = dol_t.astype(BF16)
                dol_m = jnp.concatenate([dol_b, zero] if h == 0 else [zero, dol_b], axis=0)
                for b in blocks:
                    dp = dot(block(1, b), dol_m)
                    d = pt[h, b * QB:(b + 1) * QB, rows].astype(F32) * (dp - delta)
                    ds[h, b * QB:(b + 1) * QB, rows] = d.astype(BF16)
                dqs.append(dot(kvt[0, hs, k0:k1], ds[h, k0:k1, rows]) * SCALE)
            o_ref[rows, :] = jnp.concatenate(outs, 0).T.astype(BF16)
            dq_ref[rows, :] = jnp.concatenate(dqs, 0).T.astype(BF16)
            dol = jnp.concatenate(scaled, 0).T.astype(BF16)
            for h in range(2):
                dom[h, rows, :] = jnp.where((lane < HEAD_DIM) == (h == 0), dol, jnp.zeros_like(dol))
        for b in range(base, 2 * nq):
            q0 = max(0, b - nq) * QB
            br = slice(b * QB, (b + 1) * QB)
            dk = dot(ds[0, br, q0:], qm[0, q0:, :]) + dot(ds[1, br, q0:], qm[1, q0:, :])
            dv = dot(pt[0, br, q0:], dom[0, q0:, :]) + dot(pt[1, br, q0:], dom[1, q0:, :])
            ref, i = (dkvp_ref, b) if b < nq else (dkv_ref, b - nq)
            ref[0, i * QB:(i + 1) * QB, :] = dk.astype(BF16)
            ref[1, i * QB:(i + 1) * QB, :] = dv.astype(BF16)

    @pl.when(flag_ref[0] == 1)
    def _():
        run(True)

    @pl.when(flag_ref[0] == 0)
    def _():
        run(False)
        dkvp_ref[...] = jnp.zeros_like(dkvp_ref)


def attend(flag, q, kv, kvp, do, first, pairs):
    rows = q.shape[0]
    width = pairs * PAIR
    tok_in = pl.BlockSpec((rows, PAIR), lambda i, f: (0, first + i))
    kv_in = pl.BlockSpec((2, rows, PAIR), lambda i, f: (0, 0, first + i))
    tok_out = pl.BlockSpec((rows, PAIR), lambda i, f: (0, i))
    kv_out = pl.BlockSpec((2, rows, PAIR), lambda i, f: (0, 0, i))
    tok_shape = jax.ShapeDtypeStruct((rows, width), BF16)
    kv_shape = jax.ShapeDtypeStruct((2, rows, width), BF16)
    return pl.pallas_call(
        attend_kernel,
        out_shape=(tok_shape, tok_shape, kv_shape, kv_shape),
        grid_spec=pltpu.PrefetchScalarGridSpec(
            num_scalar_prefetch=1,
            grid=(pairs,),
            in_specs=[tok_in, kv_in, kv_in, tok_in],
            out_specs=(tok_out, tok_out, kv_out, kv_out),
            scratch_shapes=[
                pltpu.VMEM((2, 2 * rows, rows), BF16),
                pltpu.VMEM((2, 2 * rows, rows), BF16),
                pltpu.VMEM((2, PAIR, 2 * rows), BF16),
                pltpu.VMEM((2, rows, PAIR), BF16),
                pltpu.VMEM((2, rows, PAIR), BF16),
            ],
        ),
        compiler_params=params(),
        cost_estimate=cost(60 * rows * rows * width, 20 * rows * width),
        name="attend",
    )(flag, q, kv, kvp, do)


def qkv_back_kernel(last, x_ref, gain_ref, shift_ref, w_ref, ang_ref, dq_ref, dkv_ref, dkvn_ref, *rest):
    if last:
        (fg_in, og_ref, part_ref, dw_ref, db_ref, ig_ref, dgain_ref, dshift_ref,
         norm, norm_t, tab, fg) = rest
    else:
        dw_ref, db_ref, fg_ref, norm, norm_t, tab, fg = rest
    step = pl.program_id(0)

    @pl.when(step == 0)
    def _():
        norm_rows(x_ref, gain_ref, shift_ref, norm)
        norm_t[...] = norm[...].T
        build_tables(ang_ref, tab)
        if last:
            fg[...] = fg_in[...]
        else:
            fg[...] = jnp.zeros_like(fg)

    blocks = []
    for n in range(STEP_PAIRS):
        mine = slice(n * PAIR, (n + 1) * PAIR)
        dq = turn(dq_ref[:, mine].astype(F32), tab, -1.0)
        dk = turn(dkv_ref[0, :, mine].astype(F32) + dkvn_ref[0, :, mine].astype(F32), tab, -1.0)
        dv = dkv_ref[1, :, mine].astype(F32) + dkvn_ref[1, :, mine].astype(F32)
        low = low_lanes(dq.shape)
        dk = pltpu.roll(dk, HEAD_DIM, 1)
        blocks += [jnp.where(low, dq, dk), jnp.where(low, dv, dq), jnp.where(low, dk, dv)]
    dm = jnp.concatenate(blocks, axis=1).astype(BF16)
    db_ref[...] = jnp.sum(dm.astype(F32), axis=0, keepdims=True)
    dw_ref[...] = dot(norm_t[...], dm).astype(BF16)
    fg[...] += dot_t(dm, w_ref[...])

    @pl.when(step == pl.num_programs(0) - 1)
    def _():
        if last:
            def emit(rows, part):
                total = og_ref[rows, :].astype(F32) + part + part_ref[rows, :]
                ig_ref[rows, :] = total.astype(BF16)

            norm_back(x_ref, gain_ref, fg, dgain_ref, dshift_ref, emit)
        else:
            fg_ref[...] = fg[...]


def qkv_back(x, gain, shift, w, ang, dq, dkv, dkvn, first, carry):
    rows, width = x.shape
    last = carry is not None
    pairs = dq.shape[1] // PAIR
    full, vec = whole((rows, width)), whole((1, width))
    wide = STEP_PAIRS * PAIR
    steps = pairs // STEP_PAIRS
    cols = 3 * wide
    tok = pl.BlockSpec((rows, wide), lambda i: (0, i))
    kvs = pl.BlockSpec((2, rows, wide), lambda i: (0, 0, i))
    outs = [jax.ShapeDtypeStruct((width, steps * cols), BF16), jax.ShapeDtypeStruct((1, steps * cols), F32)]
    specs = [pl.BlockSpec((width, cols), lambda i: (0, i)), pl.BlockSpec((1, cols), lambda i: (0, i))]
    if last:
        outs += [jax.ShapeDtypeStruct((rows, width), BF16)] + [jax.ShapeDtypeStruct((1, width), F32)] * 2
        specs += [full, vec, vec]
    else:
        outs += [jax.ShapeDtypeStruct((rows, width), F32)]
        specs += [full]
    return pl.pallas_call(
        partial(qkv_back_kernel, last),
        grid=(steps,),
        out_shape=tuple(outs),
        in_specs=[full, vec, vec, pl.BlockSpec((width, cols), lambda i: (0, first // STEP_PAIRS + i)),
                  whole(ang.shape), tok, kvs, kvs] + ([full] * 3 if last else []),
        out_specs=tuple(specs),
        scratch_shapes=[pltpu.VMEM((rows, width), BF16), pltpu.VMEM((width, rows), BF16),
                        pltpu.VMEM((3, rows, PAIR), F32), pltpu.VMEM((rows, width), F32)],
        compiler_params=params(),
        cost_estimate=cost(4 * rows * width * steps * cols, 8 * rows * width),
        name="qkv_back",
    )(x, gain, shift, w, ang, dq, dkv, dkvn, *(carry or ()))


def dense_kernel(o0_ref, o1_ref, wd_ref, db_ref, rb_ref, mid_ref, x_ref, og_ref, out_ref, dwd_ref, ot):
    half = o0_ref.shape[1]

    @pl.when(pl.program_id(0) == 0)
    def _():
        ot[:half, :] = o0_ref[...].T
        ot[half:, :] = o1_ref[...].T

    total = x_ref[...].astype(F32) + mid_ref[...] + (db_ref[...] + rb_ref[...])
    total += dot(o0_ref[...], wd_ref[:half, :]) + dot(o1_ref[...], wd_ref[half:, :])
    out_ref[...] = total.astype(BF16)
    dwd_ref[...] = dot(ot[...], og_ref[...]).astype(BF16)


def dense(o0, o1, wd, db, rb, mid, x, og):
    rows, width = x.shape
    blk = 256
    col = lambda r: pl.BlockSpec((r, blk), lambda i: (0, i))
    return pl.pallas_call(
        dense_kernel,
        grid=(width // blk,),
        out_shape=(jax.ShapeDtypeStruct((rows, width), BF16), jax.ShapeDtypeStruct((width, width), BF16)),
        in_specs=[whole(o0.shape), whole(o1.shape), col(width), col(1), col(1), col(rows), col(rows), col(rows)],
        out_specs=(col(rows), col(width)),
        scratch_shapes=[pltpu.VMEM((width, rows), BF16)],
        compiler_params=params(),
        cost_estimate=cost(4 * rows * width * width, 12 * rows * width),
        name="dense",
    )(o0, o1, wd, db, rb, mid, x, og)


MESH = pl.DeviceIdType.MESH


def scatter_kernel(bits, parts, chunks, vec_sizes, *refs):
    nvec, nmat, nchunk = len(vec_sizes), 3, len(chunks)
    mats, vecs = refs[:nmat], refs[nmat:nmat + nvec]
    outs, vec_out = refs[nmat + nvec:2 * nmat + nvec], refs[2 * nmat + nvec]
    refs = refs[2 * nmat + nvec + 1:]
    recv = [refs[c * (bits + 1):(c + 1) * (bits + 1)] for c in range(nchunk)]
    state, vrecv, send_sem, recv_sem = refs[nchunk * (bits + 1):]
    me_b, me_s = lax.axis_index("batch"), lax.axis_index("seq")
    bit = [lax.rem(me_b // (1 << k), 2) for k in range(bits)]
    mate = [(me_b + (1 << k) - 2 * (1 << k) * bit[k], me_s) for k in range(bits)]
    others = [lax.rem(me_s + d, parts) for d in range(1, parts)]
    peers = mate + [(me_b, o) for o in others]
    npeer = len(peers)

    barrier = pltpu.get_barrier_semaphore()
    for peer in peers:
        pl.semaphore_signal(barrier, inc=1, device_id=peer, device_id_type=MESH)
    pl.semaphore_wait(barrier, npeer)

    copies = {}

    def send(key, slot, n, src, dst, peer):
        copy = pltpu.make_async_remote_copy(
            src_ref=src, dst_ref=dst, send_sem=send_sem.at[slot, n], recv_sem=recv_sem.at[slot, n],
            device_id=peer, device_id_type=MESH)
        copy.start()
        copies[key, n] = copy

    def open_bits(order, stage):
        return [d for d in range(bits - 1, -1, -1) if d not in order[:stage]]

    def start(c, stage):
        mat, col, size, order = chunks[c]
        if stage == bits:
            for n, o in enumerate(others):
                send(c, c, bits + n, recv[c][bits - 1].at[o], recv[c][bits].at[n], (me_b, o))
            return
        k = order[stage]
        index = tuple(1 - bit[k] if d == k else slice(None) for d in open_bits(order, stage))
        if stage == 0:
            src = mats[mat].at[index + (slice(None), slice(None), pl.ds(col, size))]
        else:
            src = recv[c][stage - 1].at[index]
        send(c, c, stage, src, recv[c][stage], mate[k])

    def add(c, stage):
        mat, col, size, order = chunks[c]
        k = order[stage]
        dims = open_bits(order, stage)
        copies[c, stage].wait_recv()
        dst = recv[c][stage]
        lead = bits - 1 - stage

        def one(i, carry):
            part = lax.rem(i, parts)
            rest = i // parts
            sub = tuple(lax.rem(rest // (1 << (lead - 1 - n)), 2) for n in range(lead))
            left = list(sub)
            own_at = tuple(bit[k] if d == k else left.pop(0) for d in dims) + (part,)
            if stage == 0:
                own = mats[mat][own_at + (slice(None), pl.ds(col, size))]
            else:
                own = recv[c][stage - 1][own_at]
            at = sub + (part,)
            dst[at] = (own.astype(F32) + dst[at].astype(F32)).astype(BF16)
            return carry

        lax.fori_loop(0, parts << lead, one, 0)

    def finish(c):
        mat, col, size, _ = chunks[c]
        total = recv[c][bits - 1][me_s].astype(F32)
        for n in range(parts - 1):
            copies[c, bits + n].wait_recv()
            total = total + recv[c][bits][n].astype(F32)
        outs[mat][:, col:col + size] = total

    def vec_start(stage):
        if stage < bits:
            send("v", nchunk, stage, state.at[stage], vrecv.at[stage], mate[stage])
        else:
            for n, o in enumerate(others):
                send("v", nchunk, bits + n, state.at[bits], vrecv.at[bits + n], (me_b, o))

    def vec_add(stage):
        if stage < bits:
            copies["v", stage].wait_recv()
            state[stage + 1] = state[stage] + vrecv[stage]
            vec_start(stage + 1)
        else:
            total = state[bits]
            for n in range(parts - 1):
                copies["v", bits + n].wait_recv()
                total = total + vrecv[bits + n]
            vec_out[...] = total

    for c in range(nchunk):
        start(c, 0)
    at = 0
    for ref, n in zip(vecs, vec_sizes):
        state[0, :, at:at + n] = ref[...]
        at += n
    vec_start(0)
    for stage in range(bits + 1):
        for c in range(nchunk):
            if stage < bits:
                add(c, stage)
                start(c, stage + 1)
            else:
                finish(c)
        vec_add(stage)
    for copy in copies.values():
        copy.wait_send()


def scatter(bits, parts, mats, vecs):
    shards = parts << bits
    rows = mats[0].shape[0] // shards
    widths = [m.shape[1] for m in mats]
    shaped = [m.reshape((2,) * bits + (parts, rows, m.shape[1])) for m in mats]
    plain = list(range(bits))
    other = [0] + [k for i in range(1, bits, 2) for k in reversed(range(i, min(i + 2, bits)))]
    chunks = []
    for m, w in enumerate(widths):
        chunks += [(m, 0, w // 2, plain), (m, w // 2, w // 2, other)]
    vec_sizes = [v.shape[1] for v in vecs]
    total = sum(vec_sizes)
    npeer = bits + parts - 1
    scratch = []
    for _, _, size, _ in chunks:
        for stage in range(bits):
            scratch.append(pltpu.VMEM((2,) * (bits - 1 - stage) + (parts, rows, size), BF16))
        scratch.append(pltpu.VMEM((parts - 1, rows, size), BF16))
    scratch += [
        pltpu.VMEM((bits + 1, 1, total), F32),
        pltpu.VMEM((npeer, 1, total), F32),
        pltpu.SemaphoreType.DMA((len(chunks) + 1, npeer)),
        pltpu.SemaphoreType.DMA((len(chunks) + 1, npeer)),
    ]
    vmem = pl.BlockSpec(memory_space=pltpu.VMEM)
    return pl.pallas_call(
        partial(scatter_kernel, bits, parts, chunks, vec_sizes),
        out_shape=tuple(jax.ShapeDtypeStruct((rows, w), F32) for w in widths)
        + (jax.ShapeDtypeStruct((1, total), F32),),
        in_specs=[vmem] * (len(mats) + len(vecs)),
        out_specs=tuple([vmem] * (len(mats) + 1)),
        scratch_shapes=scratch,
        compiler_params=pltpu.CompilerParams(
            vmem_limit_bytes=VMEM_LIMIT, collective_id=0, has_side_effects=True),
        name="scatter",
    )(*shaped, *vecs)


def body(
    tokens,
    seq_lengths,
    attn_gain,
    attn_shift,
    qkv_weight,
    qkv_bias,
    dense_weight,
    dense_bias,
    mlp_gain,
    mlp_shift,
    expand_weight,
    expand_bias,
    reduce_weight,
    reduce_bias,
    out_grad,
):
    seq_parts = lax.axis_size("seq")
    place = lax.axis_index("seq")
    rows, width = tokens.shape
    lengths = seq_lengths[0]
    starts = jnp.cumsum(lengths) - lengths
    row0 = place * rows
    offset = row0 - jnp.max(jnp.where(starts <= row0, starts, 0))
    flag = (offset > 0).astype(jnp.int32).reshape(1)
    positions = (offset + jnp.arange(rows, dtype=jnp.int32)).astype(F32)
    frequency = jnp.exp(jnp.arange(ROT // 2, dtype=F32) * (-2.0 * math.log(10000.0) / ROT))
    phases = frequency[:, None] * positions[None, :]
    ang = jnp.concatenate([jnp.cos(phases), jnp.sin(phases)], axis=0)

    row = lambda v: v.reshape(1, -1)
    ag, ash, mg, msh = row(attn_gain), row(attn_shift), row(mlp_gain), row(mlp_shift)
    onward = [(i, i + 1) for i in range(seq_parts - 1)]
    back = [(i + 1, i) for i in range(seq_parts - 1)]

    batch_parts = lax.axis_size("batch")
    ndev = batch_parts * seq_parts
    both = ("batch", "seq")
    q, kv, do = project(tokens, ag, ash, qkv_weight, row(qkv_bias), ang, out_grad, dense_weight)
    kvp = lax.ppermute(kv, "seq", onward)
    mid, slope, dwr, dog = mlp_fwd(
        ndev, tokens, mg, msh, expand_weight, row(expand_bias), reduce_weight, out_grad)
    dwr = lax.psum_scatter(dwr, both, scatter_dimension=0, tiled=True)
    part, dwe, dbe, dmg, dms = mlp_back(
        tokens, mg, msh, expand_weight, reduce_weight, out_grad, slope)
    dwe = lax.psum_scatter(dwe, both, scatter_dimension=0, tiled=True)

    hp = width // PAIR // 2
    o0, dq0, dkv0, dkvp0 = attend(flag, q, kv, kvp, do, 0, hp)
    dkvn0 = lax.ppermute(dkvp0, "seq", back)
    o1, dq1, dkv1, dkvp1 = attend(flag, q, kv, kvp, do, hp, hp)
    dkvn1 = lax.ppermute(dkvp1, "seq", back)
    dw0, db0, fg = qkv_back(tokens, ag, ash, qkv_weight, ang, dq0, dkv0, dkvn0, 0, None)
    layer_out, dwd = dense(o0, o1, dense_weight, row(dense_bias), row(reduce_bias), mid, tokens, out_grad)
    dw1, db1, input_grad, dag, das = qkv_back(
        tokens, ag, ash, qkv_weight, ang, dq1, dkv1, dkvn1, hp, (fg, out_grad, part))
    bits = batch_parts.bit_length() - 1
    vecs = [dag, das, db0, db1, dog, dmg, dms, dbe]
    dw0, dw1, dwd, vsum = scatter(bits, seq_parts, [dw0, dw1, dwd], vecs)
    index = lax.axis_index("batch") * seq_parts + place
    pieces, at = [], 0
    for size in (width, width, 3 * width, width, width, width, dbe.shape[1]):
        own = size // ndev
        pieces.append(lax.dynamic_slice(vsum, (0, at + index * own), (1, own)).reshape(own))
        at += size
    dag, das, dqb, dog, dmg, dms, dbe = pieces
    hidden = expand_weight.shape[1]
    dwe = dwe[:, :hidden].astype(F32)
    dwr = jnp.concatenate([dwr[:, j * width:(j + 1) * width] for j in range(hidden // width)], axis=0).astype(F32)
    return (
        layer_out,
        input_grad,
        dag,
        das,
        jnp.concatenate([dw0, dw1], axis=1),
        dqb,
        dwd,
        dog,
        dmg,
        dms,
        dwe,
        dbe,
        dwr,
        dog,
    )


def solution(mesh):
    tok = P(("batch", "seq"), None)
    vec = P(("batch", "seq"))
    in_specs = (tok, P("batch", None)) + (P(),) * 12 + (tok,)
    out_specs = (tok, tok, vec, vec, tok, vec, tok, vec, vec, vec, tok, vec, tok, vec)
    return jax.shard_map(body, mesh=mesh, in_specs=in_specs, out_specs=out_specs, check_vma=False)
```

profile of v0, /device:TPU:0, one launch (start us, length us, event | category | flops | bytes accessed | tf_op | source)
XLA Modules:
  0.0 537.6 jit_solution(12129250457140817192)
XLA Ops:
  7.2 51.4 %mlp_fwd.1 = (f32[1024,1024]{1,0:T(8,128)}, bf16[1024,4096]{1,0:T(8,128)(2,1)}, bf16[1024,4224]{1,0:T(8,128)(2,1)}, f32[1,1024]{1,0:T(1,128)}) custom-call(bf16[1024,1024]{1,0:T(8,128)(2,1)} %x_ref.11, f32[1,1024]{1,0:T(1,128)} %bitcast.45, f32[1,1024]{1,0:T(1,128)} %bitcast.47, bf16[1024,4096]{1,0:T(8,128)(2,1)} %we_ref.3, f32[1,4096]{1,0:T(1,128)} %bitcast.43, ...), custom_call_target="tpu_custom_call" | custom-call | flops 25769803776 | bytes 33554432 | tf_op jit(solution)/shard_map/mlp_fwd/pallas_call | solution.py:241
  61.0 0.6 pad_maximum_fusion.1.ang_ref
  61.6 19.3 %project.1 = (bf16[1024,1024]{1,0:T(8,128)(2,1)}, bf16[2,1024,1024]{2,1,0:T(8,128)(2,1)}, bf16[1024,1024]{1,0:T(8,128)(2,1)}) custom-call(bf16[1024,1024]{1,0:T(8,128)(2,1)} %x_ref.11, f32[1,1024]{1,0:T(1,128)} %bitcast.36, f32[1,1024]{1,0:T(1,128)} %bitcast.39, bf16[1024,3072]{1,0:T(8,128)(2,1)} %w_ref.5, f32[1,3072]{1,0:T(1,128)} %bitcast.44, ...), custom_call_target="tpu_custom_call" | custom-call | flops 8589934592 | bytes 25165824 | tf_op jit(solution)/shard_map/project/pallas_call | solution.py:134
  81.0 6.9 %collective-permute-start = (bf16[2,1024,1024]{2,1,0:T(8,128)(2,1)}, bf16[2,1024,1024]{2,1,0:T(8,128)(2,1)}, u32[]{:S(2)}, u32[]{:S(2)}) collective-permute-start(bf16[2,1024,1024]{2,1,0:T(8,128)(2,1)} %get-tuple-element.49.kv_ref), channel_id=1, source_target_pairs={{0,1},{1,2},{2,3},{4,5},{5,6},{6,7},{8,9},{9,10},{10,11},{12,13},{... | collective-permute-start | bytes 12582920 | tf_op jit(solution)/shard_map/ppermute | solution.py:696
  87.9 41.4 %mlp_back.1 = (f32[1024,1024]{1,0:T(8,128)}, bf16[1024,4224]{1,0:T(8,128)(2,1)}, f32[1,4096]{1,0:T(1,128)}, f32[1,1024]{1,0:T(1,128)}, f32[1,1024]{1,0:T(1,128)}) custom-call(bf16[1024,1024]{1,0:T(8,128)(2,1)} %x_ref.11, f32[1,1024]{1,0:T(1,128)} %bitcast.46, f32[1,1024]{1,0:T(1,128)} %bitcast.48, bf16[1024,4096]{1,0:T(8,128)(2,1)} %we_ref.3, ...), custom_call_target="tpu_custom_call" | custom-call | flops 25769803776 | bytes 33554432 | tf_op jit(solution)/shard_map/mlp_back/pallas_call | solution.py:260
  129.3 85.8 %collective-permute-done.kvp_ref = bf16[2,1024,1024]{2,1,0:T(8,128)(2,1)} collective-permute-done((bf16[2,1024,1024]{2,1,0:T(8,128)(2,1)}, bf16[2,1024,1024]{2,1,0:T(8,128)(2,1)}, u32[]{:S(2)}, u32[]{:S(2)}) %collective-permute-start) | collective-permute-done | bytes 4194336 | tf_op jit(solution)/shard_map/ppermute | solution.py:696
  215.2 47.2 %attend.2 = (bf16[1024,512]{1,0:T(8,128)(2,1)}, bf16[1024,512]{1,0:T(8,128)(2,1)}, bf16[2,1024,512]{2,1,0:T(8,128)(2,1)}, bf16[2,1024,512]{2,1,0:T(8,128)(2,1)}) custom-call(s32[1]{0:T(128)} %bitcast.3.flag_ref, bf16[1024,1024]{1,0:T(8,128)(2,1)} %get-tuple-element.48.q_ref, bf16[2,1024,1024]{2,1,0:T(8,128)(2,1)} %get-tuple-element.49.kv_ref, ...), custom_call_target="tpu_custom_call" | custom-call | flops 32212254720 | bytes 10485760 | tf_op jit(solution)/shard_map/attend/pallas_call | solution.py:371
  262.4 1.3 collective-permute-start.2
  263.7 47.5 %attend.3 = (bf16[1024,512]{1,0:T(8,128)(2,1)}, bf16[1024,512]{1,0:T(8,128)(2,1)}, bf16[2,1024,512]{2,1,0:T(8,128)(2,1)}, bf16[2,1024,512]{2,1,0:T(8,128)(2,1)}) custom-call(s32[1]{0:T(128)} %bitcast.3.flag_ref, bf16[1024,1024]{1,0:T(8,128)(2,1)} %get-tuple-element.48.q_ref, bf16[2,1024,1024]{2,1,0:T(8,128)(2,1)} %get-tuple-element.49.kv_ref, ...), custom_call_target="tpu_custom_call" | custom-call | flops 32212254720 | bytes 10485760 | tf_op jit(solution)/shard_map/attend/pallas_call | solution.py:371
  311.2 1.3 collective-permute-start.1
  312.5 10.7 %dense.1 = (bf16[1024,1024]{1,0:T(8,128)(2,1)}, bf16[1024,1024]{1,0:T(8,128)(2,1)}) custom-call(bf16[1024,512]{1,0:T(8,128)(2,1)} %get-tuple-element.51.o0_ref, bf16[1024,512]{1,0:T(8,128)(2,1)} %get-tuple-element.52.o1_ref, bf16[1024,1024]{1,0:T(8,128)(2,1)} %wd_ref.3, f32[1,1024]{1,0:T(1,128)} %bitcast.49, f32[1,1024]{1,0:T(1,128)} %bitcast.50, ...), custom_call_target="tpu_custom_call" | custom-call | flops 4294967296 | bytes 12582912 | tf_op jit(solution)/shard_map/dense/pallas_call | solution.py:488
  323.2 17.8 %qkv_back.2 = (bf16[1024,1536]{1,0:T(8,128)(2,1)}, f32[1,1536]{1,0:T(1,128)}, f32[1024,1024]{1,0:T(8,128)}) custom-call(bf16[1024,1024]{1,0:T(8,128)(2,1)} %x_ref.11, f32[1,1024]{1,0:T(1,128)} %bitcast.37, f32[1,1024]{1,0:T(1,128)} %bitcast.40, bf16[1024,3072]{1,0:T(8,128)(2,1)} %w_ref.5, f32[16,1024]{1,0:T(8,128)} %pad_maximum_fusion.1.ang_ref, ...), custom_call_target="tpu_custom_call" | custom-call | flops 6442450944 | bytes 8388608 | tf_op jit(solution)/shard_map/qkv_back/pallas_call | solution.py:455
  341.0 35.5 %collective-permute-done.1.dkvn_ref = bf16[2,1024,512]{2,1,0:T(8,128)(2,1)S(1)} collective-permute-done((bf16[2,1024,512]{2,1,0:T(8,128)(2,1)}, bf16[2,1024,512]{2,1,0:T(8,128)(2,1)S(1)}, u32[]{:S(2)}, u32[]{:S(2)}) %collective-permute-start.1) | collective-permute-done | bytes 2097184 | tf_op jit(solution)/shard_map/ppermute | solution.py:708
  376.5 1.3 copy-done
  377.8 23.6 %qkv_back.3 = (bf16[1024,1536]{1,0:T(8,128)(2,1)}, f32[1,1536]{1,0:T(1,128)}, bf16[1024,1024]{1,0:T(8,128)(2,1)}, f32[1,1024]{1,0:T(1,128)}, f32[1,1024]{1,0:T(1,128)}) custom-call(bf16[1024,1024]{1,0:T(8,128)(2,1)} %x_ref.11, f32[1,1024]{1,0:T(1,128)} %bitcast.38, f32[1,1024]{1,0:T(1,128)} %bitcast.41, bf16[1024,3072]{1,0:T(8,128)(2,1)} %w_ref.5, ...), custom_call_target="tpu_custom_call" | custom-call | flops 6442450944 | bytes 8388608 | tf_op jit(solution)/shard_map/qkv_back/pallas_call | solution.py:455
  401.4 118.7 %scatter.1 = (f32[32,1536]{1,0:T(8,128)}, f32[32,1536]{1,0:T(8,128)}, f32[32,1024]{1,0:T(8,128)}, f32[1,12288]{1,0:T(1,128)}) custom-call(bf16[2,2,2,4,32,1536]{5,4,3,2,1,0:T(8,128)(2,1)} %bitcast.33, bf16[2,2,2,4,32,1536]{5,4,3,2,1,0:T(8,128)(2,1)} %bitcast.34, bf16[2,2,2,4,32,1024]{5,4,3,2,1,0:T(8,128)(2,1)} %bitcast.35, ...), custom_call_target="tpu_custom_call" | custom-call | tf_op jit(solution)/shard_map/scatter/pallas_call | solution.py:644
  520.1 1.3 fusion.5
  521.5 1.2 fusion.2
  522.6 1.1 fusion.6
  523.8 1.8 pad_maximum_fusion
  525.6 1.0 fusion.8
  526.5 0.8 maximum_convert_fusion
  527.4 1.8 slice_convert_fusion
  529.7 0.7 copy.32
  (20 shorter events, 2.2 us)
Async XLA Ops:
  7.2 518.4 %reduce-scatter.5.cloned.1.call-start = ((), (), s32[]{:S(2)}) async-start(), calls=%async_computation.3 | async-start | bytes 8921088 | tf_op jit(solution)/shard_map/reduce_scatter | solution.py:699
  58.7 0.7 copy-start.2
  58.7 468.7 %reduce-scatter.3.cloned.1.call-start = ((), (), s32[]{:S(2)}) async-start(), calls=%async_computation.2 | async-start | bytes 8921088 | tf_op jit(solution)/shard_map/reduce_scatter | solution.py:702
  81.0 134.2 %collective-permute-start = (bf16[2,1024,1024]{2,1,0:T(8,128)(2,1)}, bf16[2,1024,1024]{2,1,0:T(8,128)(2,1)}, u32[]{:S(2)}, u32[]{:S(2)}) collective-permute-start(bf16[2,1024,1024]{2,1,0:T(8,128)(2,1)} %get-tuple-element.49.kv_ref), channel_id=1, source_target_pairs={{0,1},{1,2},{2,3},{4,5},{5,6},{6,7},{8,9},{9,10},{10,11},{12,13},{... | collective-permute-start | bytes 12582920 | tf_op jit(solution)/shard_map/ppermute | solution.py:696
  262.4 60.8 %collective-permute-start.2 = (bf16[2,1024,512]{2,1,0:T(8,128)(2,1)}, bf16[2,1024,512]{2,1,0:T(8,128)(2,1)}, u32[]{:S(2)}, u32[]{:S(2)}) collective-permute-start(bf16[2,1024,512]{2,1,0:T(8,128)(2,1)} %get-tuple-element.60), channel_id=1, source_target_pairs={{1,0},{2,1},{3,2},{5,4},{6,5},{7,6},{9,8},{10,9},{11,10},{13,12},{... | collective-permute-start | bytes 6291464 | tf_op jit(solution)/shard_map/ppermute | solution.py:706
  311.2 65.3 %collective-permute-start.1 = (bf16[2,1024,512]{2,1,0:T(8,128)(2,1)}, bf16[2,1024,512]{2,1,0:T(8,128)(2,1)S(1)}, u32[]{:S(2)}, u32[]{:S(2)}) collective-permute-start(bf16[2,1024,512]{2,1,0:T(8,128)(2,1)} %get-tuple-element.57), channel_id=1, source_target_pairs={{1,0},{2,1},{3,2},{5,4},{6,5},{7,6},{9,8},{10,9},{11,10},{13,12},{... | collective-permute-start | bytes 6291464 | tf_op jit(solution)/shard_map/ppermute | solution.py:708
  376.5 1.3 copy-start
  520.1 9.6 %copy-start.1 = (f32[32,1024]{1,0:T(8,128)S(1)}, f32[32,1024]{1,0:T(8,128)}, u32[]{:S(2)}) copy-start(f32[32,1024]{1,0:T(8,128)} %get-tuple-element.141) | copy-start | bytes 393220
  521.5 8.9 %copy-start.3 = (f32[32]{0:T(128)}, f32[32]{0:T(128)S(1)}, u32[]{:S(2)}) copy-start(f32[32]{0:T(128)S(1)} %get-tuple-element.142) | copy-start | bytes 388
Sparse Core Ops, SparseCore 0:
  58.8 162.2 reduce-scatter.4
  227.0 149.2 reduce-scatter.2
where the time goes:
time: 546 us; the launch traced here: 538 us
  Pallas kernels  378 us (69%)
  waiting for transfers between devices  121 us (22%)
  between operations  15.2 us (3%)
  starting transfers between devices  9.83 us (2%)
  local copies, waits for them, and re-layouts  7.41 us (1%)
  other arithmetic  6.08 us (1%)
    pallas_call x1, Pallas kernels, scatter(): pl.pallas_call(partial(scatter_kernel, bits, parts, chunks, vec_sizes), o...  119 us
    pallas_call x2, Pallas kernels, attend(): pl.pallas_call(attend_kernel, out_shape=(tok_shape, tok_shape, kv_shape,...  94.8 us
    ppermute x1, waiting for transfers between devices, body(): kvp = lax.ppermute(kv, 'seq', onward)  85.8 us
    pallas_call x1, Pallas kernels, mlp_fwd(): pl.pallas_call(partial(mlp_fwd_kernel, out_rows // ndev), grid=(hidden //...  51.4 us
    pallas_call x1, Pallas kernels, mlp_back(): pl.pallas_call(mlp_back_kernel, grid=(hidden // FB,), out_shape=(jax.Shap...  41.4 us
    pallas_call x2, Pallas kernels, qkv_back(): pl.pallas_call(partial(qkv_back_kernel, last), grid=(steps,), out_shape=t...  41.4 us
    ppermute x1, waiting for transfers between devices, body(): dkvn1 = lax.ppermute(dkvp1, 'seq', back)  35.5 us
    pallas_call x1, Pallas kernels, project(): pl.pallas_call(project_kernel, grid=(width // wide,), out_shape=(jax.Shap...  19.3 us
  transfers between devices with their start and end apart: 5, of which 2 were waited for; matrix products, arithmetic and copies ran while one was open for 2% of the time, Pallas kernels for 61%

commit v1 on v0

v1 whole, which is shorter than its diff:
```python
from functools import partial
import math

import jax
import jax.numpy as jnp
from jax import lax
from jax.experimental import pallas as pl
from jax.experimental.pallas import tpu as pltpu
from jax.sharding import PartitionSpec as P


HEAD_DIM = 64
ROT = 16
PAIR = 2 * HEAD_DIM
EPSILON = 1e-05
MASKED = -1e30
SCALE = 1.0 / math.sqrt(HEAD_DIM)
QB = 256
FB = 1024
STEP_PAIRS = 2
ROWS = 128
F32 = jnp.float32
BF16 = jnp.bfloat16
VMEM_LIMIT = 60 << 20


def dot(left, right):
    return jnp.dot(left, right, preferred_element_type=F32)


def dot_t(left, right):
    return lax.dot_general(left, right, (((1,), (1,)), ((), ())), preferred_element_type=F32)


def params():
    return pltpu.CompilerParams(vmem_limit_bytes=VMEM_LIMIT)


def cost(flops, nbytes):
    return pl.CostEstimate(flops=int(flops), bytes_accessed=int(nbytes), transcendentals=0)


def whole(shape):
    return pl.BlockSpec(shape, lambda i: (0,) * len(shape), pipeline_mode=pl.Buffered(1))


def statistics(x):
    mean = jnp.mean(x, axis=-1, keepdims=True)
    centered = x - mean
    variance = jnp.mean(centered * centered, axis=-1, keepdims=True)
    rstd = lax.rsqrt(variance + EPSILON)
    return centered * rstd, rstd


def norm_rows(x_ref, gain_ref, shift_ref, out_ref):
    def step(i, carry):
        rows = pl.ds(pl.multiple_of(i * ROWS, ROWS), ROWS)
        xn, _ = statistics(x_ref[rows, :].astype(F32))
        out_ref[rows, :] = (xn * gain_ref[...] + shift_ref[...]).astype(BF16)
        return carry

    lax.fori_loop(0, x_ref.shape[0] // ROWS, step, 0)


def norm_back(x_ref, gain_ref, grad_ref, gaingrad_ref, shiftgrad_ref, emit):
    gaingrad_ref[...] = jnp.zeros_like(gaingrad_ref)
    shiftgrad_ref[...] = jnp.zeros_like(shiftgrad_ref)

    def step(i, carry):
        rows = pl.ds(pl.multiple_of(i * ROWS, ROWS), ROWS)
        xn, rstd = statistics(x_ref[rows, :].astype(F32))
        grad = grad_ref[rows, :]
        gaingrad_ref[...] += jnp.sum(grad * xn, axis=0, keepdims=True)
        shiftgrad_ref[...] += jnp.sum(grad, axis=0, keepdims=True)
        scaled = grad * gain_ref[...]
        mean_s = jnp.mean(scaled, axis=-1, keepdims=True)
        mean_sx = jnp.mean(scaled * xn, axis=-1, keepdims=True)
        emit(rows, rstd * (scaled - mean_s - xn * mean_sx))
        return carry

    lax.fori_loop(0, x_ref.shape[0] // ROWS, step, 0)


def build_tables(angle_ref, tab_ref):
    half = ROT // 2
    cos8, sin8 = angle_ref[0:half, :], angle_ref[half:ROT, :]
    rest = HEAD_DIM - ROT
    count = cos8.shape[1]
    ones = jnp.ones((rest, count), F32)
    zeros = jnp.zeros((rest, count), F32)
    z8 = jnp.zeros_like(sin8)
    tab_ref[0] = jnp.concatenate([cos8, cos8, ones] * 2, axis=0).T
    tab_ref[1] = jnp.concatenate([-sin8, z8, zeros] * 2, axis=0).T
    tab_ref[2] = jnp.concatenate([z8, sin8, zeros] * 2, axis=0).T


def turn(u, tab_ref, sign):
    half = ROT // 2
    ahead = pltpu.roll(u, PAIR - half, 1)
    behind = pltpu.roll(u, half, 1)
    return u * tab_ref[0] + sign * (ahead * tab_ref[1] + behind * tab_ref[2])


def low_lanes(shape):
    return lax.broadcasted_iota(jnp.int32, shape, 1) < HEAD_DIM


def project_kernel(x_ref, gain_ref, shift_ref, w_ref, b_ref, ang_ref, og_ref, wd_ref,
                   q_ref, kv_ref, do_ref, norm, tab):
    @pl.when(pl.program_id(0) == 0)
    def _():
        norm_rows(x_ref, gain_ref, shift_ref, norm)
        build_tables(ang_ref, tab)

    for n in range(STEP_PAIRS):
        cols = slice(n * 3 * PAIR, (n + 1) * 3 * PAIR)
        mine = slice(n * PAIR, (n + 1) * PAIR)
        mixed = dot(norm[...], w_ref[:, cols]) + b_ref[:, cols]
        t0, t1, t2 = mixed[:, :PAIR], mixed[:, PAIR:2 * PAIR], mixed[:, 2 * PAIR:]
        low = low_lanes(t0.shape)
        q = jnp.where(low, t0, t1)
        k = pltpu.roll(jnp.where(low, t2, t0), HEAD_DIM, 1)
        v = jnp.where(low, t1, t2)
        q_ref[:, mine] = turn(q, tab, 1.0).astype(BF16)
        kv_ref[0, :, mine] = turn(k, tab, 1.0).astype(BF16)
        kv_ref[1, :, mine] = v.astype(BF16)
    do_ref[...] = dot_t(og_ref[...], wd_ref[...]).astype(BF16)


def project(x, gain, shift, w, b, ang, og, wd):
    rows, width = x.shape
    wide = STEP_PAIRS * PAIR
    tok = pl.BlockSpec((rows, wide), lambda i: (0, i))
    return pl.pallas_call(
        project_kernel,
        grid=(width // wide,),
        out_shape=(
            jax.ShapeDtypeStruct((rows, width), BF16),
            jax.ShapeDtypeStruct((2, rows, width), BF16),
            jax.ShapeDtypeStruct((rows, width), BF16),
        ),
        in_specs=[
            whole((rows, width)), whole((1, width)), whole((1, width)),
            pl.BlockSpec((width, 3 * wide), lambda i: (0, i)),
            pl.BlockSpec((1, 3 * wide), lambda i: (0, i)),
            whole(ang.shape), whole((rows, width)),
            pl.BlockSpec((wide, width), lambda i: (i, 0)),
        ],
        out_specs=(tok, pl.BlockSpec((2, rows, wide), lambda i: (0, 0, i)), tok),
        scratch_shapes=[pltpu.VMEM((rows, width), BF16), pltpu.VMEM((3, rows, PAIR), F32)],
        compiler_params=params(),
        cost_estimate=cost(8 * rows * width * width, 24 * rows * width),
        name="project",
    )(x, gain, shift, w, b, ang, og, wd)


def gelu_parts(h):
    z = jnp.abs(h) * math.sqrt(0.5)
    t = 1.0 / (1.0 + 0.5 * z)
    poly = jnp.full_like(t, 0.17087277)
    for c in (-0.82215223, 1.48851587, -1.13520398, 0.27886807, -0.18628806, 0.09678418,
              0.37409196, 1.00002368, -1.26551223):
        poly = poly * t + c
    zz = z * z
    tail = 0.5 * t * jnp.exp(poly - zz)
    cdf = jnp.where(h >= 0, 1.0 - tail, tail)
    slope = cdf + h * (jnp.exp(-zz) * (1.0 / math.sqrt(2.0 * math.pi)))
    return h * cdf, slope


def mlp_fwd_kernel(take, x_ref, gain_ref, shift_ref, we_ref, be_ref, wr_ref, og_ref,
                   mid_ref, slope_ref, dwr_ref, dog_ref, norm):
    step = pl.program_id(0)
    width = x_ref.shape[1]

    @pl.when(step == 0)
    def _():
        norm_rows(x_ref, gain_ref, shift_ref, norm)
        mid_ref[...] = jnp.zeros_like(mid_ref)
        dog_ref[...] = jnp.sum(og_ref[...].astype(F32), axis=0, keepdims=True)

    h = dot(norm[...], we_ref[...]) + be_ref[...]
    active, slope = gelu_parts(h)
    active = active.astype(BF16)
    slope_ref[...] = slope.astype(BF16)
    mid_ref[...] += dot(active, wr_ref[...])
    dwr = dot(active.T, og_ref[...]).astype(BF16)
    full = dwr_ref.shape[1]
    ratio = full // width
    for piece in range(FB // take):
        group, j = piece // ratio, piece % ratio
        dwr_ref[group * take:(group + 1) * take, j * width:(j + 1) * width] = (
            dwr[piece * take:(piece + 1) * take, :])


def mlp_back_kernel(x_ref, gain_ref, shift_ref, we_ref, wr_ref, og_ref, slope_ref,
                    part_ref, dwe_ref, dbe_ref, dgain_ref, dshift_ref, norm, norm_t, sg):
    step = pl.program_id(0)

    @pl.when(step == 0)
    def _():
        norm_rows(x_ref, gain_ref, shift_ref, norm)
        norm_t[...] = norm[...].T
        sg[...] = jnp.zeros_like(sg)

    hidden = (dot_t(og_ref[...], wr_ref[...]) * slope_ref[...].astype(F32)).astype(BF16)
    dwe_ref[...] = dot(norm_t[...], hidden).astype(BF16)
    dbe_ref[...] = jnp.sum(hidden.astype(F32), axis=0, keepdims=True)
    sg[...] += dot_t(hidden, we_ref[...])

    @pl.when(step == pl.num_programs(0) - 1)
    def _():
        def emit(rows, part):
            part_ref[rows, :] = part

        norm_back(x_ref, gain_ref, sg, dgain_ref, dshift_ref, emit)


def mlp_specs(x):
    rows, width = x.shape
    full = whole((rows, width))
    vec = whole((1, width))
    up = pl.BlockSpec((width, FB), lambda i: (0, i))
    down = pl.BlockSpec((FB, width), lambda i: (i, 0))
    bias = pl.BlockSpec((1, FB), lambda i: (0, i))
    act = pl.BlockSpec((rows, FB), lambda i: (0, i))
    return full, vec, up, down, bias, act


def mlp_fwd(ndev, x, gain, shift, we, be, wr, og):
    rows, width = x.shape
    hidden = we.shape[1]
    full, vec, up, down, bias, act = mlp_specs(x)
    out_rows = hidden // (hidden // width)
    blk = FB * out_rows // hidden
    gshape = (out_rows, hidden)
    return pl.pallas_call(
        partial(mlp_fwd_kernel, out_rows // ndev),
        grid=(hidden // FB,),
        out_shape=(jax.ShapeDtypeStruct((rows, width), F32), jax.ShapeDtypeStruct((rows, hidden), BF16),
                   jax.ShapeDtypeStruct(gshape, BF16), jax.ShapeDtypeStruct((1, width), F32)),
        in_specs=[full, vec, vec, up, bias, down, full],
        out_specs=(full, act, pl.BlockSpec((blk, gshape[1]), lambda i: (i, 0)), vec),
        scratch_shapes=[pltpu.VMEM((rows, width), BF16)],
        compiler_params=params(),
        cost_estimate=cost(6 * rows * width * hidden, 8 * width * hidden),
        name="mlp_fwd",
    )(x, gain, shift, we, be, wr, og)


def mlp_back(x, gain, shift, we, wr, og, slope):
    rows, width = x.shape
    hidden = we.shape[1]
    full, vec, up, down, bias, act = mlp_specs(x)
    vshape = jax.ShapeDtypeStruct((1, width), F32)
    return pl.pallas_call(
        mlp_back_kernel,
        grid=(hidden // FB,),
        out_shape=(jax.ShapeDtypeStruct((rows, width), F32),
                   jax.ShapeDtypeStruct((width, hidden), BF16),
                   jax.ShapeDtypeStruct((1, hidden), F32), vshape, vshape),
        in_specs=[full, vec, vec, up, down, full, act],
        out_specs=(full, up, bias, vec, vec),
        scratch_shapes=[pltpu.VMEM((rows, width), BF16), pltpu.VMEM((width, rows), BF16),
                        pltpu.VMEM((rows, width), F32)],
        compiler_params=params(),
        cost_estimate=cost(6 * rows * width * hidden, 8 * width * hidden),
        name="mlp_back",
    )(x, gain, shift, we, wr, og, slope)


MESH = pl.DeviceIdType.MESH


class Halving:
    def __init__(self, bits, parts, chunks, mats, own, recv, send_sem, recv_sem):
        self.bits, self.parts, self.chunks = bits, parts, chunks
        self.mats, self.own, self.recv = mats, own, recv
        self.send_sem, self.recv_sem = send_sem, recv_sem
        self.me_b, self.me_s = lax.axis_index("batch"), lax.axis_index("seq")
        self.bit = [lax.rem(self.me_b // (1 << k), 2) for k in range(bits)]
        self.mate = [
            (self.me_b + (1 << k) - 2 * (1 << k) * self.bit[k], self.me_s) for k in range(bits)]
        self.others = [(self.me_b, lax.rem(self.me_s + d, parts)) for d in range(1, parts)]
        self.peers = self.mate + self.others

    def barrier(self):
        sem = pltpu.get_barrier_semaphore()
        for peer in self.peers:
            pl.semaphore_signal(sem, inc=1, device_id=peer, device_id_type=MESH)
        pl.semaphore_wait(sem, len(self.peers))

    def copy(self, slot, n, src, dst, peer):
        return pltpu.make_async_remote_copy(
            src_ref=src, dst_ref=dst, send_sem=self.send_sem.at[slot, n],
            recv_sem=self.recv_sem.at[slot, n], device_id=peer, device_id_type=MESH)

    def dims(self, order, stage):
        return [d for d in range(self.bits - 1, -1, -1) if d not in order[:stage]]

    def part(self, c, value):
        mat, col, size, order = self.chunks[c]
        index = tuple(value if d == order[0] else slice(None) for d in self.dims(order, 0))
        return self.mats[mat].at[index + (slice(None), slice(None), pl.ds(col, size))]

    def copies(self, c, stage):
        order = self.chunks[c][3]
        if stage == self.bits:
            return [
                self.copy(c, self.bits + n, self.recv[c][stage - 1].at[peer[1]], self.recv[c][stage].at[n], peer)
                for n, peer in enumerate(self.others)]
        k = order[stage]
        if stage == 0:
            src = self.part(c, 1 - self.bit[k])
        else:
            index = tuple(1 - self.bit[k] if d == k else slice(None) for d in self.dims(order, stage))
            src = self.recv[c][stage - 1].at[index]
        return [self.copy(c, stage, src, self.recv[c][stage], self.mate[k])]

    def start(self, c, stage):
        for copy in self.copies(c, stage):
            copy.start()

    def wait_sends(self, c):
        for stage in range(self.bits + 1):
            for copy in self.copies(c, stage):
                copy.wait_send()

    def add(self, c, stage):
        mat, col, size, order = self.chunks[c]
        k = order[stage]
        dims = self.dims(order, stage)
        self.copies(c, stage)[0].wait_recv()
        dst = self.recv[c][stage]
        lead = self.bits - 1 - stage

        def one(i, carry):
            part = lax.rem(i, self.parts)
            rest = i // self.parts
            sub = tuple(lax.rem(rest // (1 << (lead - 1 - n)), 2) for n in range(lead))
            at = sub + (part,)
            left = list(sub)
            own_at = tuple(self.bit[k] if d == k else left.pop(0) for d in dims) + (part,)
            if stage > 0:
                own = self.recv[c][stage - 1][own_at]
            elif self.own is None:
                own = self.mats[mat][own_at + (slice(None), pl.ds(col, size))]
            else:
                own = self.own[c][at]
            dst[at] = (own.astype(F32) + dst[at].astype(F32)).astype(BF16)
            return carry

        lax.fori_loop(0, self.parts << lead, one, 0)

    def total(self, c):
        total = self.recv[c][self.bits - 1][self.me_s].astype(F32)
        for n, copy in enumerate(self.copies(c, self.bits)):
            copy.wait_recv()
            total = total + self.recv[c][self.bits][n].astype(F32)
        return total


def halving_orders(bits):
    plain = list(range(bits))
    other = [0] + [k for i in range(1, bits, 2) for k in reversed(range(i, min(i + 2, bits)))]
    return plain, other


def halving_scratch(bits, parts, rows, chunks):
    scratch = []
    for _, _, size, _ in chunks:
        for stage in range(bits):
            scratch.append(pltpu.VMEM((2,) * (bits - 1 - stage) + (parts, rows, size), BF16))
        scratch.append(pltpu.VMEM((parts - 1, rows, size), BF16))
    return scratch


def attend_pair(flag_ref, q_ref, kv_ref, kvp_ref, do_ref, o_ref, dq_ref, dkv_ref, dkvp_ref,
                pt, ds, kvt, qm, dom):
    rows_all = q_ref.shape[0]
    nq = rows_all // QB
    away = (flag_ref[0] - 1).astype(F32) * (-MASKED)
    sources = [(kvp_ref, i) for i in range(nq)] + [(kv_ref, i) for i in range(nq)]

    def block(which, b):
        ref, i = sources[b]
        return ref[which, i * QB:(i + 1) * QB, :]

    for which in range(2):
        kvt[which, :, :rows_all] = kvp_ref[which].T
        kvt[which, :, rows_all:] = kv_ref[which].T
    lane = lax.broadcasted_iota(jnp.int32, (QB, PAIR), 1)
    sub = lax.broadcasted_iota(jnp.int32, (PAIR, QB), 0)
    causal = lax.broadcasted_iota(jnp.int32, (QB, QB), 0) <= lax.broadcasted_iota(
        jnp.int32, (QB, QB), 1)
    for j in range(nq):
        rows = slice(j * QB, (j + 1) * QB)
        q = q_ref[rows, :] * jnp.asarray(SCALE, BF16)
        qt = q.T
        dot_rows = do_ref[rows, :].astype(F32).T
        blocks = range(nq + j + 1)
        k1 = (nq + j + 1) * QB
        outs, scaled, dqs = [], [], []
        for h in range(2):
            hs = slice(h * HEAD_DIM, (h + 1) * HEAD_DIM)
            qm[h, rows, :] = jnp.where((lane < HEAD_DIM) == (h == 0), q, jnp.zeros_like(q))
            qtm = jnp.where((sub < HEAD_DIM) == (h == 0), qt, jnp.zeros_like(qt))
            scores, tops = [], [None, None]
            for b in blocks:
                s = dot(block(0, b), qtm)
                if b == nq + j:
                    s = jnp.where(causal, s, MASKED)
                scores.append(s)
                part = jnp.max(s.reshape(QB // 8, 8, QB), axis=0)
                side = int(b >= nq)
                tops[side] = part if tops[side] is None else jnp.maximum(tops[side], part)
            top = jnp.max(jnp.maximum(tops[0] + away, tops[1]), axis=0, keepdims=True)
            shift = (top - away, top)
            total = None
            for b, s in zip(blocks, scores):
                p = jnp.exp(s - shift[int(b >= nq)])
                part = jnp.sum(p.reshape(QB // 8, 8, QB), axis=0)
                total = part if total is None else total + part
                pt[h, b * QB:(b + 1) * QB, rows] = p.astype(BF16)
            inv = 1.0 / jnp.sum(total, axis=0, keepdims=True)
            out_t = dot(kvt[1, hs, :k1], pt[h, :k1, rows]) * inv
            dol_t = dot_rows[hs] * inv
            delta = jnp.sum(dol_t * out_t, axis=0, keepdims=True)
            outs.append(out_t)
            scaled.append(dol_t)
            zero = jnp.zeros((HEAD_DIM, QB), BF16)
            dol_b = dol_t.astype(BF16)
            dol_m = jnp.concatenate([dol_b, zero] if h == 0 else [zero, dol_b], axis=0)
            for b in blocks:
                dp = dot(block(1, b), dol_m)
                d = pt[h, b * QB:(b + 1) * QB, rows].astype(F32) * (dp - delta)
                ds[h, b * QB:(b + 1) * QB, rows] = d.astype(BF16)
            dqs.append(dot(kvt[0, hs, :k1], ds[h, :k1, rows]) * SCALE)
        o_ref[rows, :] = jnp.concatenate(outs, 0).T.astype(BF16)
        dq_ref[rows, :] = jnp.concatenate(dqs, 0).T.astype(BF16)
        dol = jnp.concatenate(scaled, 0).T.astype(BF16)
        for h in range(2):
            dom[h, rows, :] = jnp.where((lane < HEAD_DIM) == (h == 0), dol, jnp.zeros_like(dol))
    for b in range(2 * nq):
        q0 = max(0, b - nq) * QB
        br = slice(b * QB, (b + 1) * QB)
        dk = dot(ds[0, br, q0:], qm[0, q0:, :]) + dot(ds[1, br, q0:], qm[1, q0:, :])
        dv = dot(pt[0, br, q0:], dom[0, q0:, :]) + dot(pt[1, br, q0:], dom[1, q0:, :])
        ref, i = (dkvp_ref, b) if b < nq else (dkv_ref, b - nq)
        ref[0, i * QB:(i + 1) * QB, :] = dk.astype(BF16)
        ref[1, i * QB:(i + 1) * QB, :] = dv.astype(BF16)


def attend_kernel(bits, parts, chunks, flag_ref, q_ref, kv_ref, kvp_ref, do_ref, gw_ref, gr_ref,
                  o_ref, dq_ref, dkv_ref, dkvn_ref, outw_ref, outr_ref, *refs):
    nchunk = len(chunks)
    own, refs = refs[:nchunk], refs[nchunk:]
    recv = [refs[c * (bits + 1):(c + 1) * (bits + 1)] for c in range(nchunk)]
    (pt, ds, kvt, qm, dom, back, own_sem, send_sem, recv_sem, back_send, back_recv) = refs[
        nchunk * (bits + 1):]
    red = Halving(bits, parts, chunks, (gw_ref, gr_ref), own, recv, send_sem, recv_sem)
    step = pl.program_id(0)
    steps = dkvn_ref.shape[2] // PAIR

    def own_copy(c):
        return pltpu.make_async_copy(red.part(c, red.bit[chunks[c][3][0]]), own[c], own_sem.at[c])

    def back_copy(i):
        cols = pl.ds(pl.multiple_of(i * PAIR, PAIR), PAIR)
        return pltpu.make_async_remote_copy(
            src_ref=back.at[lax.rem(i, 2)], dst_ref=dkvn_ref.at[:, :, cols],
            send_sem=back_send.at[i], recv_sem=back_recv.at[i],
            device_id=red.others[parts - 2], device_id_type=MESH)

    @pl.when(step == 0)
    def _():
        red.barrier()
        for c in range(nchunk):
            red.start(c, 0)
        for c in range(nchunk):
            own_copy(c).start()

    moments = [max(1, steps * m // 8) for m in (1, 4, 6)]
    moments += [moments[-1]] * (bits - 3)
    for stage in range(bits):
        @pl.when(step == moments[stage])
        def _(stage=stage):
            for c in range(nchunk):
                if stage == 0:
                    own_copy(c).wait()
                red.add(c, stage)
                red.start(c, stage + 1)

    @pl.when(step >= 2)
    def _():
        back_copy(step - 2).wait_send()

    attend_pair(flag_ref, q_ref, kv_ref, kvp_ref, do_ref, o_ref, dq_ref, dkv_ref,
                back.at[lax.rem(step, 2)], pt, ds, kvt, qm, dom)
    back_copy(step).start()

    @pl.when(step == steps - 1)
    def _():
        rows = outw_ref.shape[0]
        width = outr_ref.shape[1]
        for c in range(nchunk):
            mat, col, size, _ = chunks[c]
            total = red.total(c)
            if mat == 0:
                outw_ref[:, col:col + size] = total
            else:
                for n in range(size // width):
                    j = col // width + n
                    outr_ref[j * rows:(j + 1) * rows, :] = total[:, n * width:(n + 1) * width]
        for c in range(nchunk):
            red.wait_sends(c)
        for i in range(max(0, steps - 2), steps):
            back_copy(i).wait_send()
        for i in range(steps):
            back_copy(i).wait_recv()


def attend(bits, parts, flag, q, kv, kvp, do, gw, gr):
    rows, width = q.shape
    steps = width // PAIR
    hidden = gw.shape[1]
    take = gw.shape[0] // (parts << bits)
    shaped = [g.reshape((2,) * bits + (parts, take, hidden)) for g in (gw, gr)]
    plain, other = halving_orders(bits)
    chunks = [(0, 0, hidden // 2, plain), (1, 0, hidden // 2, other),
              (0, hidden // 2, hidden // 2, plain), (1, hidden // 2, hidden // 2, other)]
    npeer = bits + parts - 1
    tok = pl.BlockSpec((rows, PAIR), lambda i: (0, i))
    kvs = pl.BlockSpec((2, rows, PAIR), lambda i: (0, 0, i))
    hbm = pl.BlockSpec(memory_space=pl.ANY)
    tok_shape = jax.ShapeDtypeStruct((rows, width), BF16)
    kv_shape = jax.ShapeDtypeStruct((2, rows, width), BF16)
    fold = hidden // width
    outw, outr = (take, hidden), (take * fold, width)
    return pl.pallas_call(
        partial(attend_kernel, bits, parts, chunks),
        grid=(steps,),
        out_shape=(tok_shape, tok_shape, kv_shape, kv_shape,
                   jax.ShapeDtypeStruct(outw, F32), jax.ShapeDtypeStruct(outr, F32)),
        in_specs=[pl.BlockSpec(memory_space=pltpu.SMEM), tok, kvs, kvs, tok, hbm, hbm],
        out_specs=(tok, tok, kvs, hbm, whole(outw), whole(outr)),
        scratch_shapes=[
            pltpu.VMEM((2,) * (bits - 1) + (parts, take, size), BF16) for _, _, size, _ in chunks
        ] + halving_scratch(bits, parts, take, chunks) + [
            pltpu.VMEM((2, 2 * rows, rows), BF16),
            pltpu.VMEM((2, 2 * rows, rows), BF16),
            pltpu.VMEM((2, PAIR, 2 * rows), BF16),
            pltpu.VMEM((2, rows, PAIR), BF16),
            pltpu.VMEM((2, rows, PAIR), BF16),
            pltpu.VMEM((2, 2, rows, PAIR), BF16),
            pltpu.SemaphoreType.DMA((len(chunks),)),
            pltpu.SemaphoreType.DMA((len(chunks), npeer)),
            pltpu.SemaphoreType.DMA((len(chunks), npeer)),
            pltpu.SemaphoreType.DMA((steps,)),
            pltpu.SemaphoreType.DMA((steps,)),
        ],
        compiler_params=pltpu.CompilerParams(
            vmem_limit_bytes=63 << 20, collective_id=1, has_side_effects=True),
        cost_estimate=cost(60 * rows * rows * width, 20 * rows * width),
        name="attend",
    )(flag, q, kv, kvp, do, *shaped)


def qkv_back_kernel(x_ref, gain_ref, shift_ref, w_ref, ang_ref, dq_ref, dkv_ref, dkvn_ref,
                    og_ref, part_ref, dw_ref, db_ref, ig_ref, dgain_ref, dshift_ref,
                    norm, norm_t, tab, fg):
    step = pl.program_id(0)

    @pl.when(step == 0)
    def _():
        norm_rows(x_ref, gain_ref, shift_ref, norm)
        norm_t[...] = norm[...].T
        build_tables(ang_ref, tab)
        fg[...] = jnp.zeros_like(fg)

    blocks = []
    for n in range(STEP_PAIRS):
        mine = slice(n * PAIR, (n + 1) * PAIR)
        dq = turn(dq_ref[:, mine].astype(F32), tab, -1.0)
        dk = turn(dkv_ref[0, :, mine].astype(F32) + dkvn_ref[0, :, mine].astype(F32), tab, -1.0)
        dv = dkv_ref[1, :, mine].astype(F32) + dkvn_ref[1, :, mine].astype(F32)
        low = low_lanes(dq.shape)
        dk = pltpu.roll(dk, HEAD_DIM, 1)
        blocks += [jnp.where(low, dq, dk), jnp.where(low, dv, dq), jnp.where(low, dk, dv)]
    dm = jnp.concatenate(blocks, axis=1).astype(BF16)
    db_ref[...] = jnp.sum(dm.astype(F32), axis=0, keepdims=True)
    dw_ref[...] = dot(norm_t[...], dm).astype(BF16)
    fg[...] += dot_t(dm, w_ref[...])

    @pl.when(step == pl.num_programs(0) - 1)
    def _():
        def emit(rows, part):
            total = og_ref[rows, :].astype(F32) + part + part_ref[rows, :]
            ig_ref[rows, :] = total.astype(BF16)

        norm_back(x_ref, gain_ref, fg, dgain_ref, dshift_ref, emit)


def qkv_back(x, gain, shift, w, ang, dq, dkv, dkvn, og, part):
    rows, width = x.shape
    full, vec = whole((rows, width)), whole((1, width))
    wide = STEP_PAIRS * PAIR
    cols = 3 * wide
    tok = pl.BlockSpec((rows, wide), lambda i: (0, i))
    kvs = pl.BlockSpec((2, rows, wide), lambda i: (0, 0, i))
    up, bias = pl.BlockSpec((width, cols), lambda i: (0, i)), pl.BlockSpec((1, cols), lambda i: (0, i))
    vshape = jax.ShapeDtypeStruct((1, width), F32)
    return pl.pallas_call(
        qkv_back_kernel,
        grid=(width // wide,),
        out_shape=(jax.ShapeDtypeStruct((width, 3 * width), BF16), jax.ShapeDtypeStruct((1, 3 * width), F32),
                   jax.ShapeDtypeStruct((rows, width), BF16), vshape, vshape),
        in_specs=[full, vec, vec, up, whole(ang.shape), tok, kvs, kvs, full, full],
        out_specs=(up, bias, full, vec, vec),
        scratch_shapes=[pltpu.VMEM((rows, width), BF16), pltpu.VMEM((width, rows), BF16),
                        pltpu.VMEM((3, rows, PAIR), F32), pltpu.VMEM((rows, width), F32)],
        compiler_params=params(),
        cost_estimate=cost(12 * rows * width * width, 8 * rows * width),
        name="qkv_back",
    )(x, gain, shift, w, ang, dq, dkv, dkvn, og, part)


def dense_kernel(o_ref, wd_ref, db_ref, rb_ref, mid_ref, x_ref, og_ref, out_ref, dwd_ref, ot):
    @pl.when(pl.program_id(0) == 0)
    def _():
        ot[...] = o_ref[...].T

    total = x_ref[...].astype(F32) + mid_ref[...] + (db_ref[...] + rb_ref[...])
    out_ref[...] = (total + dot(o_ref[...], wd_ref[...])).astype(BF16)
    dwd_ref[...] = dot(ot[...], og_ref[...]).astype(BF16)


def dense(o, wd, db, rb, mid, x, og):
    rows, width = x.shape
    blk = 256
    col = lambda r: pl.BlockSpec((r, blk), lambda i: (0, i))
    return pl.pallas_call(
        dense_kernel,
        grid=(width // blk,),
        out_shape=(jax.ShapeDtypeStruct((rows, width), BF16), jax.ShapeDtypeStruct((width, width), BF16)),
        in_specs=[whole(o.shape), col(width), col(1), col(1), col(rows), col(rows), col(rows)],
        out_specs=(col(rows), col(width)),
        scratch_shapes=[pltpu.VMEM((width, rows), BF16)],
        compiler_params=params(),
        cost_estimate=cost(4 * rows * width * width, 12 * rows * width),
        name="dense",
    )(o, wd, db, rb, mid, x, og)


def scatter_kernel(bits, parts, nmat, chunks, vec_sizes, *refs):
    nvec, nchunk = len(vec_sizes), len(chunks)
    mats, vecs = refs[:nmat], refs[nmat:nmat + nvec]
    outs, vec_out = refs[nmat + nvec:2 * nmat + nvec], refs[2 * nmat + nvec]
    refs = refs[2 * nmat + nvec + 1:]
    recv = [refs[c * (bits + 1):(c + 1) * (bits + 1)] for c in range(nchunk)]
    state, vrecv, send_sem, recv_sem = refs[nchunk * (bits + 1):]
    red = Halving(bits, parts, chunks, mats, None, recv, send_sem, recv_sem)
    red.barrier()
    for c in range(nchunk):
        red.start(c, 0)
    at = 0
    for ref, n in zip(vecs, vec_sizes):
        state[0, :, at:at + n] = ref[...]
        at += n

    def vec_copies(stage):
        if stage < bits:
            return [red.copy(nchunk, stage, state.at[stage], vrecv.at[stage], red.mate[stage])]
        return [red.copy(nchunk, bits + n, state.at[bits], vrecv.at[bits + n], peer)
                for n, peer in enumerate(red.others)]

    def vec_start(stage):
        for copy in vec_copies(stage):
            copy.start()

    def vec_add(stage):
        copies = vec_copies(stage)
        for copy in copies:
            copy.wait_recv()
        total = state[stage]
        for n in range(len(copies)):
            total = total + vrecv[stage + n]
        if stage < bits:
            state[stage + 1] = total
            vec_start(stage + 1)
        else:
            vec_out[...] = total

    vec_start(0)
    for stage in range(bits + 1):
        for c in range(nchunk):
            if stage < bits:
                red.add(c, stage)
                red.start(c, stage + 1)
            else:
                mat, col, size, _ = chunks[c]
                outs[mat][:, col:col + size] = red.total(c)
        vec_add(stage)
    for c in range(nchunk):
        red.wait_sends(c)
    for stage in range(bits + 1):
        for copy in vec_copies(stage):
            copy.wait_send()


def scatter(bits, parts, mats, vecs):
    shards = parts << bits
    rows = mats[0].shape[0] // shards
    widths = [m.shape[1] for m in mats]
    shaped = [m.reshape((2,) * bits + (parts, rows, m.shape[1])) for m in mats]
    plain, other = halving_orders(bits)
    chunks = []
    for m, w in enumerate(widths):
        size = w // 4 if w > 2048 else w // 2
        for n in range(w // size):
            chunks.append((m, n * size, size, other if n % 2 else plain))
    vec_sizes = [v.shape[1] for v in vecs]
    total = sum(vec_sizes)
    npeer = bits + parts - 1
    scratch = halving_scratch(bits, parts, rows, chunks) + [
        pltpu.VMEM((bits + 1, 1, total), F32),
        pltpu.VMEM((npeer, 1, total), F32),
        pltpu.SemaphoreType.DMA((len(chunks) + 1, npeer)),
        pltpu.SemaphoreType.DMA((len(chunks) + 1, npeer)),
    ]
    vmem = pl.BlockSpec(memory_space=pltpu.VMEM)
    return pl.pallas_call(
        partial(scatter_kernel, bits, parts, len(mats), chunks, vec_sizes),
        out_shape=tuple(jax.ShapeDtypeStruct((rows, w), F32) for w in widths)
        + (jax.ShapeDtypeStruct((1, total), F32),),
        in_specs=[vmem] * (len(mats) + len(vecs)),
        out_specs=tuple([vmem] * (len(mats) + 1)),
        scratch_shapes=scratch,
        compiler_params=pltpu.CompilerParams(
            vmem_limit_bytes=VMEM_LIMIT, collective_id=0, has_side_effects=True),
        name="scatter",
    )(*shaped, *vecs)


def body(
    tokens,
    seq_lengths,
    attn_gain,
    attn_shift,
    qkv_weight,
    qkv_bias,
    dense_weight,
    dense_bias,
    mlp_gain,
    mlp_shift,
    expand_weight,
    expand_bias,
    reduce_weight,
    reduce_bias,
    out_grad,
):
    seq_parts = lax.axis_size("seq")
    place = lax.axis_index("seq")
    rows, width = tokens.shape
    lengths = seq_lengths[0]
    starts = jnp.cumsum(lengths) - lengths
    row0 = place * rows
    offset = row0 - jnp.max(jnp.where(starts <= row0, starts, 0))
    flag = (offset > 0).astype(jnp.int32).reshape(1)
    positions = (offset + jnp.arange(rows, dtype=jnp.int32)).astype(F32)
    frequency = jnp.exp(jnp.arange(ROT // 2, dtype=F32) * (-2.0 * math.log(10000.0) / ROT))
    phases = frequency[:, None] * positions[None, :]
    ang = jnp.concatenate([jnp.cos(phases), jnp.sin(phases)], axis=0)

    row = lambda v: v.reshape(1, -1)
    ag, ash, mg, msh = row(attn_gain), row(attn_shift), row(mlp_gain), row(mlp_shift)
    onward = [(i, i + 1) for i in range(seq_parts - 1)]

    batch_parts = lax.axis_size("batch")
    ndev = batch_parts * seq_parts
    bits = batch_parts.bit_length() - 1
    q, kv, do = project(tokens, ag, ash, qkv_weight, row(qkv_bias), ang, out_grad, dense_weight)
    kvp = lax.ppermute(kv, "seq", onward)
    mid, slope, dwr, dog = mlp_fwd(
        ndev, tokens, mg, msh, expand_weight, row(expand_bias), reduce_weight, out_grad)
    part, dwe, dbe, dmg, dms = mlp_back(
        tokens, mg, msh, expand_weight, reduce_weight, out_grad, slope)

    o, dq, dkv, dkvn, dwe, dwr = attend(bits, seq_parts, flag, q, kv, kvp, do, dwe, dwr)
    layer_out, dwd = dense(o, dense_weight, row(dense_bias), row(reduce_bias), mid, tokens, out_grad)
    dw, db, input_grad, dag, das = qkv_back(
        tokens, ag, ash, qkv_weight, ang, dq, dkv, dkvn, out_grad, part)
    vecs = [dag, das, db, dog, dmg, dms, dbe]
    dw, dwd, vsum = scatter(bits, seq_parts, [dw, dwd], vecs)
    index = lax.axis_index("batch") * seq_parts + place
    pieces, at = [], 0
    for size in (width, width, 3 * width, width, width, width, dbe.shape[1]):
        own = size // ndev
        pieces.append(lax.dynamic_slice(vsum, (0, at + index * own), (1, own)).reshape(own))
        at += size
    dag, das, dqb, dog, dmg, dms, dbe = pieces
    return (
        layer_out,
        input_grad,
        dag,
        das,
        dw,
        dqb,
        dwd,
        dog,
        dmg,
        dms,
        dwe,
        dbe,
        dwr,
        dog,
    )


def solution(mesh):
    tok = P(("batch", "seq"), None)
    vec = P(("batch", "seq"))
    in_specs = (tok, P("batch", None)) + (P(),) * 12 + (tok,)
    out_specs = (tok, tok, vec, vec, tok, vec, tok, vec, vec, vec, tok, vec, tok, vec)
    return jax.shard_map(body, mesh=mesh, in_specs=in_specs, out_specs=out_specs, check_vma=False)
```

time: 546 us -> 434 us (0.79)
  waiting for transfers between devices: 121 us -> 0.01 us
  Pallas kernels: 378 us -> 409 us
  between operations: 15.2 us -> 1.62 us
    ppermute x1, waiting for transfers between devices: 85.8 us -> 0.01 us  [body(): kvp = lax.ppermute(kv, 'seq', onward)]
    ppermute x2 -> x0, waiting for transfers between devices: 35.5 us -> none  [the longest x1 35.5 us: body(): dkvn1 = lax.ppermute(dkvp1, 'seq', back)]
    pallas_call x5 -> x3, Pallas kernels: 255 us -> 273 us  [the longest x1 164 us: attend(): pl.pallas_call(partial(attend_kernel, bits, parts, chunks), grid=(steps,)...]
    pallas_call x1, Pallas kernels: 41.4 us -> 55.1 us  [mlp_back(): pl.pallas_call(mlp_back_kernel, grid=(hidden // FB,), out_shape=(jax.Shap...]
  transfers between devices with their start and end apart: 5 -> 1, of which waited for: 2 -> 0; matrix products, arithmetic and copies ran while one was open for 2% -> 0% of each run, Pallas kernels for 61% -> 25%
where the time goes in v1:
time: 434 us; the launch traced here: 430 us
  Pallas kernels  409 us (94%)
  local copies, waits for them, and re-layouts  9.17 us (2%)
  starting transfers between devices  7.26 us (2%)
    pallas_call x1, Pallas kernels, attend(): pl.pallas_call(partial(attend_kernel, bits, parts, chunks), grid=(steps,)...  164 us
    pallas_call x1, Pallas kernels, scatter(): pl.pallas_call(partial(scatter_kernel, bits, parts, len(mats), chunks, ve...  77.3 us
    pallas_call x1, Pallas kernels, mlp_back(): pl.pallas_call(mlp_back_kernel, grid=(hidden // FB,), out_shape=(jax.Shap...  55.1 us
    pallas_call x1, Pallas kernels, mlp_fwd(): pl.pallas_call(partial(mlp_fwd_kernel, out_rows // ndev), grid=(hidden //...  51.4 us
    pallas_call x1, Pallas kernels, qkv_back(): pl.pallas_call(qkv_back_kernel, grid=(width // wide,), out_shape=(jax.Sha...  31 us
    pallas_call x1, Pallas kernels, project(): pl.pallas_call(project_kernel, grid=(width // wide,), out_shape=(jax.Shap...  19.3 us
    pallas_call x1, Pallas kernels, dense(): pl.pallas_call(dense_kernel, grid=(width // blk,), out_shape=(jax.ShapeDt...  10.7 us
  transfers between devices with their start and end apart: 1, of which 0 were waited for; matrix products, arithmetic and copies ran while one was open for 0% of the time, Pallas kernels for 25%

profile of v1, /device:TPU:0, one launch (start us, length us, event | category | flops | bytes accessed | tf_op | source)
XLA Modules:
  0.0 430.1 jit_solution(2055944907370960970)
XLA Ops:
  0.7 0.8 reduce-window.9
  1.5 1.3 fusion.7
  3.5 0.2 multiply_cosine_fusion
  3.7 0.6 pad_maximum_fusion.ang_ref
  4.3 19.3 %project.1 = (bf16[1024,1024]{1,0:T(8,128)(2,1)}, bf16[2,1024,1024]{2,1,0:T(8,128)(2,1)}, bf16[1024,1024]{1,0:T(8,128)(2,1)}) custom-call(bf16[1024,1024]{1,0:T(8,128)(2,1)} %x_ref.9, f32[1,1024]{1,0:T(1,128)} %bitcast.43, f32[1,1024]{1,0:T(1,128)} %bitcast.45, bf16[1024,3072]{1,0:T(8,128)(2,1)} %w_ref.3, f32[1,3072]{1,0:T(1,128)} %bitcast.38, ...), custom_call_target="tpu_custom_call" | custom-call | flops 8589934592 | bytes 25165824 | tf_op jit(solution)/shard_map/project/pallas_call | solution.py:134
  23.6 7.3 %collective-permute-start = (bf16[2,1024,1024]{2,1,0:T(8,128)(2,1)}, bf16[2,1024,1024]{2,1,0:T(8,128)(2,1)}, u32[]{:S(2)}, u32[]{:S(2)}) collective-permute-start(bf16[2,1024,1024]{2,1,0:T(8,128)(2,1)} %get-tuple-element.43.kv_ref), channel_id=1, source_target_pairs={{0,1},{1,2},{2,3},{4,5},{5,6},{6,7},{8,9},{9,10},{10,11},{12,13},{... | collective-permute-start | bytes 12582920 | tf_op jit(solution)/shard_map/ppermute | solution.py:783
  30.9 51.4 %mlp_fwd.1 = (f32[1024,1024]{1,0:T(8,128)}, bf16[1024,4096]{1,0:T(8,128)(2,1)}, bf16[1024,4096]{1,0:T(8,128)(2,1)}, f32[1,1024]{1,0:T(1,128)}) custom-call(bf16[1024,1024]{1,0:T(8,128)(2,1)} %x_ref.9, f32[1,1024]{1,0:T(1,128)} %bitcast.39, f32[1,1024]{1,0:T(1,128)} %bitcast.41, bf16[1024,4096]{1,0:T(8,128)(2,1)} %we_ref.3, f32[1,4096]{1,0:T(1,128)} %bitcast.37, ...), custom_call_target="tpu_custom_call" | custom-call | flops 25769803776 | bytes 33554432 | tf_op jit(solution)/shard_map/mlp_fwd/pallas_call | solution.py:237
  82.3 55.1 %mlp_back.1 = (f32[1024,1024]{1,0:T(8,128)}, bf16[1024,4096]{1,0:T(8,128)(2,1)}, f32[1,4096]{1,0:T(1,128)}, f32[1,1024]{1,0:T(1,128)}, f32[1,1024]{1,0:T(1,128)}) custom-call(bf16[1024,1024]{1,0:T(8,128)(2,1)} %x_ref.9, f32[1,1024]{1,0:T(1,128)} %bitcast.40, f32[1,1024]{1,0:T(1,128)} %bitcast.42, bf16[1024,4096]{1,0:T(8,128)(2,1)} %we_ref.3, ...), custom_call_target="tpu_custom_call" | custom-call | flops 25769803776 | bytes 33554432 | tf_op jit(solution)/shard_map/mlp_back/pallas_call | solution.py:256
  137.4 0.0 collective-permute-done.kvp_ref
  137.4 164.3 %attend.1 = (bf16[1024,1024]{1,0:T(8,128)(2,1)}, bf16[1024,1024]{1,0:T(8,128)(2,1)}, bf16[2,1024,1024]{2,1,0:T(8,128)(2,1)}, bf16[2,1024,1024]{2,1,0:T(8,128)(2,...) custom-call(s32[1]{0:T(128)} %bitcast.3.flag_ref, bf16[1024,1024]{1,0:T(8,128)(2,1)} %get-tuple-element.42.q_ref, ...), custom_call_target="tpu_custom_call" | custom-call | flops 64424509440 | bytes 20971520 | tf_op jit(solution)/shard_map/attend/pallas_call | solution.py:540
  301.7 31.0 %qkv_back.1 = (bf16[1024,3072]{1,0:T(8,128)(2,1)}, f32[1,3072]{1,0:T(1,128)}, bf16[1024,1024]{1,0:T(8,128)(2,1)}, f32[1,1024]{1,0:T(1,128)}, f32[1,1024]{1,0:T(1,128)}) custom-call(bf16[1024,1024]{1,0:T(8,128)(2,1)} %x_ref.9, f32[1,1024]{1,0:T(1,128)} %bitcast.44, f32[1,1024]{1,0:T(1,128)} %bitcast.46, bf16[1024,3072]{1,0:T(8,128)(2,1)} %w_ref.3, ...), custom_call_target="tpu_custom_call" | custom-call | flops 12884901888 | bytes 8388608 | tf_op jit(solution)/shard_map/qkv_back/pallas_call | solution.py:613
  332.6 10.7 %dense.1 = (bf16[1024,1024]{1,0:T(8,128)(2,1)}, bf16[1024,1024]{1,0:T(8,128)(2,1)}) custom-call(bf16[1024,1024]{1,0:T(8,128)(2,1)} %get-tuple-element.48.o_ref, bf16[1024,1024]{1,0:T(8,128)(2,1)} %wd_ref.3, f32[1,1024]{1,0:T(1,128)} %bitcast.47, f32[1,1024]{1,0:T(1,128)} %bitcast.48, f32[1024,1024]{1,0:T(8,128)} %get-tuple-element.49.mid_ref, ...), custom_call_target="tpu_custom_call" | custom-call | flops 4294967296 | bytes 12582912 | tf_op jit(solution)/shard_map/dense/pallas_call | solution.py:642
  343.4 0.0 copy-start
  343.4 77.3 %scatter.1 = (f32[32,3072]{1,0:T(8,128)}, f32[32,1024]{1,0:T(8,128)}, f32[1,12288]{1,0:T(1,128)}) custom-call(bf16[2,2,2,4,32,3072]{5,4,3,2,1,0:T(8,128)(2,1)} %bitcast.34, bf16[2,2,2,4,32,1024]{5,4,3,2,1,0:T(8,128)(2,1)} %bitcast.35, f32[1,1024]{1,0:T(1,128)} %get-tuple-element.58.refs_2_, f32[1,1024]{1,0:T(1,128)} %get-tuple-element.59.refs_3_, ...), custom_call_target="tpu_custom_call" | custom-call | tf_op jit(solution)/shard_map/scatter/pallas_call | solution.py:732
  420.7 1.3 fusion.2
  422.0 1.2 fusion.6
  423.2 1.3 fusion.5
  424.4 0.5 copy.34
  424.9 1.8 copy.35
  426.7 1.6 copy.36
  428.3 0.0 copy-done.1
  428.3 0.8 copy.37
  429.1 0.8 copy.38
  429.9 0.0 copy-done.2
  (5 shorter events, 0.0 us)
Async XLA Ops:
  23.6 113.8 %collective-permute-start = (bf16[2,1024,1024]{2,1,0:T(8,128)(2,1)}, bf16[2,1024,1024]{2,1,0:T(8,128)(2,1)}, u32[]{:S(2)}, u32[]{:S(2)}) collective-permute-start(bf16[2,1024,1024]{2,1,0:T(8,128)(2,1)} %get-tuple-element.43.kv_ref), channel_id=1, source_target_pairs={{0,1},{1,2},{2,3},{4,5},{5,6},{6,7},{8,9},{9,10},{10,11},{12,13},{... | collective-permute-start | bytes 12582920 | tf_op jit(solution)/shard_map/ppermute | solution.py:783
  343.4 84.9 %copy-start.1 = (f32[32,4096]{1,0:T(8,128)S(1)}, f32[32,4096]{1,0:T(8,128)}, u32[]{:S(2)}) copy-start(f32[32,4096]{1,0:T(8,128)} %get-tuple-element.129) | copy-start | bytes 1572868
  343.4 85.7 %copy-start = (f32[128,1024]{1,0:T(8,128)S(1)}, f32[128,1024]{1,0:T(8,128)}, u32[]{:S(2)}) copy-start(f32[128,1024]{1,0:T(8,128)} %get-tuple-element.131) | copy-start | bytes 1572868
  424.4 5.4 %copy-start.2 = (f32[32]{0:T(128)}, f32[32]{0:T(128)S(1)}, u32[]{:S(2)}) copy-start(f32[32]{0:T(128)S(1)} %get-tuple-element.126) | copy-start | bytes 388

commit v2 on v1

--- a/solution.py
+++ b/solution.py
@@ -52,27 +52,34 @@
     return centered * rstd, rstd
 
 
-def norm_rows(x_ref, gain_ref, shift_ref, out_ref):
+def row_block(i):
+    return pl.ds(pl.multiple_of(i * ROWS, ROWS), ROWS)
+
+
+def norm_rows(x_ref, gains, outs):
     def step(i, carry):
-        rows = pl.ds(pl.multiple_of(i * ROWS, ROWS), ROWS)
+        rows = row_block(i)
         xn, _ = statistics(x_ref[rows, :].astype(F32))
-        out_ref[rows, :] = (xn * gain_ref[...] + shift_ref[...]).astype(BF16)
+        for (gain_ref, shift_ref), out_ref in zip(gains, outs):
+            out_ref[rows, :] = (xn * gain_ref[...] + shift_ref[...]).astype(BF16)
         return carry
 
     lax.fori_loop(0, x_ref.shape[0] // ROWS, step, 0)
 
 
-def norm_back(x_ref, gain_ref, grad_ref, gaingrad_ref, shiftgrad_ref, emit):
-    gaingrad_ref[...] = jnp.zeros_like(gaingrad_ref)
-    shiftgrad_ref[...] = jnp.zeros_like(shiftgrad_ref)
+def norm_back(x_ref, gains, grads, gain_grads, shift_grads, emit):
+    for ref in gain_grads + shift_grads:
+        ref[...] = jnp.zeros_like(ref)
 
     def step(i, carry):
-        rows = pl.ds(pl.multiple_of(i * ROWS, ROWS), ROWS)
+        rows = row_block(i)
         xn, rstd = statistics(x_ref[rows, :].astype(F32))
-        grad = grad_ref[rows, :]
-        gaingrad_ref[...] += jnp.sum(grad * xn, axis=0, keepdims=True)
-        shiftgrad_ref[...] += jnp.sum(grad, axis=0, keepdims=True)
-        scaled = grad * gain_ref[...]
+        scaled = 0.0
+        for gain_ref, grad_ref, dgain_ref, dshift_ref in zip(gains, grads, gain_grads, shift_grads):
+            grad = grad_ref[rows, :]
+            dgain_ref[...] += jnp.sum(grad * xn, axis=0, keepdims=True)
+            dshift_ref[...] += jnp.sum(grad, axis=0, keepdims=True)
+            scaled = scaled + grad * gain_ref[...]
         mean_s = jnp.mean(scaled, axis=-1, keepdims=True)
         mean_sx = jnp.mean(scaled * xn, axis=-1, keepdims=True)
         emit(rows, rstd * (scaled - mean_s - xn * mean_sx))
@@ -105,11 +112,20 @@
     return lax.broadcasted_iota(jnp.int32, shape, 1) < HEAD_DIM
 
 
-def project_kernel(x_ref, gain_ref, shift_ref, w_ref, b_ref, ang_ref, og_ref, wd_ref,
-                   q_ref, kv_ref, do_ref, norm, tab):
+def project_kernel(x_ref, gain_ref, shift_ref, gain2_ref, shift2_ref, w_ref, b_ref, ang_ref, og_ref,
+                   wd_ref, q_ref, kv_ref, do_ref, n1t_ref, n2_ref, n2t_ref,
+                   norm, n1t, n2, n2t, tab, sem):
+    saves = [pltpu.make_async_copy(src, dst, sem.at[n]) for n, (src, dst) in enumerate(
+        ((n1t, n1t_ref), (n2, n2_ref), (n2t, n2t_ref)))]
+
     @pl.when(pl.program_id(0) == 0)
     def _():
-        norm_rows(x_ref, gain_ref, shift_ref, norm)
+        norm_rows(x_ref, ((gain_ref, shift_ref), (gain2_ref, shift2_ref)), (norm, n2))
+        saves[1].start()
+        n1t[...] = norm[...].T
+        saves[0].start()
+        n2t[...] = n2[...].T
+        saves[2].start()
         build_tables(ang_ref, tab)
 
     for n in range(STEP_PAIRS):
@@ -126,8 +142,13 @@
         kv_ref[1, :, mine] = v.astype(BF16)
     do_ref[...] = dot_t(og_ref[...], wd_ref[...]).astype(BF16)
 
-
-def project(x, gain, shift, w, b, ang, og, wd):
+    @pl.when(pl.program_id(0) == pl.num_programs(0) - 1)
+    def _():
+        for save in saves:
+            save.wait()
+
+
+def project(x, gain, shift, gain2, shift2, w, b, ang, og, wd):
     rows, width = x.shape
     wide = STEP_PAIRS * PAIR
     tok = pl.BlockSpec((rows, wide), lambda i: (0, i))
@@ -138,20 +159,26 @@
             jax.ShapeDtypeStruct((rows, width), BF16),
             jax.ShapeDtypeStruct((2, rows, width), BF16),
             jax.ShapeDtypeStruct((rows, width), BF16),
+            jax.ShapeDtypeStruct((width, rows), BF16),
+            jax.ShapeDtypeStruct((rows, width), BF16),
+            jax.ShapeDtypeStruct((width, rows), BF16),
         ),
         in_specs=[
-            whole((rows, width)), whole((1, width)), whole((1, width)),
+            whole((rows, width)), *[whole((1, width))] * 4,
             pl.BlockSpec((width, 3 * wide), lambda i: (0, i)),
             pl.BlockSpec((1, 3 * wide), lambda i: (0, i)),
             whole(ang.shape), whole((rows, width)),
             pl.BlockSpec((wide, width), lambda i: (i, 0)),
         ],
-        out_specs=(tok, pl.BlockSpec((2, rows, wide), lambda i: (0, 0, i)), tok),
-        scratch_shapes=[pltpu.VMEM((rows, width), BF16), pltpu.VMEM((3, rows, PAIR), F32)],
+        out_specs=(tok, pl.BlockSpec((2, rows, wide), lambda i: (0, 0, i)), tok,
+                   *[pl.BlockSpec(memory_space=pl.ANY)] * 3),
+        scratch_shapes=[pltpu.VMEM((rows, width), BF16), pltpu.VMEM((width, rows), BF16),
+                        pltpu.VMEM((rows, width), BF16), pltpu.VMEM((width, rows), BF16),
+                        pltpu.VMEM((3, rows, PAIR), F32), pltpu.SemaphoreType.DMA((3,))],
         compiler_params=params(),
         cost_estimate=cost(8 * rows * width * width, 24 * rows * width),
         name="project",
-    )(x, gain, shift, w, b, ang, og, wd)
+    )(x, gain, shift, gain2, shift2, w, b, ang, og, wd)
 
 
 def gelu_parts(h):
@@ -168,14 +195,12 @@
     return h * cdf, slope
 
 
-def mlp_fwd_kernel(take, x_ref, gain_ref, shift_ref, we_ref, be_ref, wr_ref, og_ref,
-                   mid_ref, slope_ref, dwr_ref, dog_ref, norm):
+def mlp_fwd_kernel(take, norm, we_ref, be_ref, wr_ref, og_ref, mid_ref, slope_ref, dwr_ref, dog_ref):
     step = pl.program_id(0)
-    width = x_ref.shape[1]
+    width = norm.shape[1]
 
     @pl.when(step == 0)
     def _():
-        norm_rows(x_ref, gain_ref, shift_ref, norm)
         mid_ref[...] = jnp.zeros_like(mid_ref)
         dog_ref[...] = jnp.sum(og_ref[...].astype(F32), axis=0, keepdims=True)
 
@@ -193,27 +218,15 @@
             dwr[piece * take:(piece + 1) * take, :])
 
 
-def mlp_back_kernel(x_ref, gain_ref, shift_ref, we_ref, wr_ref, og_ref, slope_ref,
-                    part_ref, dwe_ref, dbe_ref, dgain_ref, dshift_ref, norm, norm_t, sg):
-    step = pl.program_id(0)
-
-    @pl.when(step == 0)
-    def _():
-        norm_rows(x_ref, gain_ref, shift_ref, norm)
-        norm_t[...] = norm[...].T
+def mlp_back_kernel(norm_t, we_ref, wr_ref, og_ref, slope_ref, sg, dwe_ref, dbe_ref):
+    @pl.when(pl.program_id(0) == 0)
+    def _():
         sg[...] = jnp.zeros_like(sg)
 
     hidden = (dot_t(og_ref[...], wr_ref[...]) * slope_ref[...].astype(F32)).astype(BF16)
     dwe_ref[...] = dot(norm_t[...], hidden).astype(BF16)
     dbe_ref[...] = jnp.sum(hidden.astype(F32), axis=0, keepdims=True)
     sg[...] += dot_t(hidden, we_ref[...])
-
-    @pl.when(step == pl.num_programs(0) - 1)
-    def _():
-        def emit(rows, part):
-            part_ref[rows, :] = part
-
-        norm_back(x_ref, gain_ref, sg, dgain_ref, dshift_ref, emit)
 
 
 def mlp_specs(x):
@@ -227,11 +240,11 @@
     return full, vec, up, down, bias, act
 
 
-def mlp_fwd(ndev, x, gain, shift, we, be, wr, og):
-    rows, width = x.shape
+def mlp_fwd(ndev, norm, we, be, wr, og):
+    rows, width = norm.shape
     hidden = we.shape[1]
-    full, vec, up, down, bias, act = mlp_specs(x)
-    out_rows = hidden // (hidden // width)
+    full, vec, up, down, bias, act = mlp_specs(norm)
+    out_rows = width
     blk = FB * out_rows // hidden
     gshape = (out_rows, hidden)
     return pl.pallas_call(
@@ -239,34 +252,29 @@
         grid=(hidden // FB,),
         out_shape=(jax.ShapeDtypeStruct((rows, width), F32), jax.ShapeDtypeStruct((rows, hidden), BF16),
                    jax.ShapeDtypeStruct(gshape, BF16), jax.ShapeDtypeStruct((1, width), F32)),
-        in_specs=[full, vec, vec, up, bias, down, full],
-        out_specs=(full, act, pl.BlockSpec((blk, gshape[1]), lambda i: (i, 0)), vec),
-        scratch_shapes=[pltpu.VMEM((rows, width), BF16)],
+        in_specs=[full, up, bias, down, full],
+        out_specs=(full, act, pl.BlockSpec((blk, hidden), lambda i: (i, 0)), vec),
         compiler_params=params(),
         cost_estimate=cost(6 * rows * width * hidden, 8 * width * hidden),
         name="mlp_fwd",
-    )(x, gain, shift, we, be, wr, og)
-
-
-def mlp_back(x, gain, shift, we, wr, og, slope):
-    rows, width = x.shape
+    )(norm, we, be, wr, og)
+
+
+def mlp_back(norm_t, we, wr, og, slope):
+    rows, width = og.shape
     hidden = we.shape[1]
-    full, vec, up, down, bias, act = mlp_specs(x)
-    vshape = jax.ShapeDtypeStruct((1, width), F32)
+    full, _, up, down, bias, act = mlp_specs(og)
     return pl.pallas_call(
         mlp_back_kernel,
         grid=(hidden // FB,),
-        out_shape=(jax.ShapeDtypeStruct((rows, width), F32),
-                   jax.ShapeDtypeStruct((width, hidden), BF16),
-                   jax.ShapeDtypeStruct((1, hidden), F32), vshape, vshape),
-        in_specs=[full, vec, vec, up, down, full, act],
-        out_specs=(full, up, bias, vec, vec),
-        scratch_shapes=[pltpu.VMEM((rows, width), BF16), pltpu.VMEM((width, rows), BF16),
-                        pltpu.VMEM((rows, width), F32)],
+        out_shape=(jax.ShapeDtypeStruct((rows, width), F32), jax.ShapeDtypeStruct((width, hidden), BF16),
+                   jax.ShapeDtypeStruct((1, hidden), F32)),
+        in_specs=[whole(norm_t.shape), up, down, full, act],
+        out_specs=(full, up, bias),
         compiler_params=params(),
         cost_estimate=cost(6 * rows * width * hidden, 8 * width * hidden),
         name="mlp_back",
-    )(x, gain, shift, we, wr, og, slope)
+    )(norm_t, we, wr, og, slope)
 
 
 MESH = pl.DeviceIdType.MESH
@@ -321,8 +329,8 @@
         for copy in self.copies(c, stage):
             copy.start()
 
-    def wait_sends(self, c):
-        for stage in range(self.bits + 1):
+    def wait_sends(self, c, stages):
+        for stage in range(stages):
             for copy in self.copies(c, stage):
                 copy.wait_send()
 
@@ -347,7 +355,7 @@
                 own = self.mats[mat][own_at + (slice(None), pl.ds(col, size))]
             else:
                 own = self.own[c][at]
-            dst[at] = (own.astype(F32) + dst[at].astype(F32)).astype(BF16)
+            dst[at] = own + dst[at]
             return carry
 
         lax.fori_loop(0, self.parts << lead, one, 0)
@@ -366,17 +374,18 @@
     return plain, other
 
 
-def halving_scratch(bits, parts, rows, chunks):
+def halving_scratch(bits, parts, rows, chunks, last):
     scratch = []
     for _, _, size, _ in chunks:
         for stage in range(bits):
             scratch.append(pltpu.VMEM((2,) * (bits - 1 - stage) + (parts, rows, size), BF16))
-        scratch.append(pltpu.VMEM((parts - 1, rows, size), BF16))
+        if last:
+            scratch.append(pltpu.VMEM((parts - 1, rows, size), BF16))
     return scratch
 
 
 def attend_pair(flag_ref, q_ref, kv_ref, kvp_ref, do_ref, o_ref, dq_ref, dkv_ref, dkvp_ref,
-                pt, ds, kvt, qm, dom):
+                pt, ds, kvt, qm, dom, midway):
     rows_all = q_ref.shape[0]
     nq = rows_all // QB
     away = (flag_ref[0] - 1).astype(F32) * (-MASKED)
@@ -394,6 +403,8 @@
     causal = lax.broadcasted_iota(jnp.int32, (QB, QB), 0) <= lax.broadcasted_iota(
         jnp.int32, (QB, QB), 1)
     for j in range(nq):
+        if j == nq // 2:
+            midway()
         rows = slice(j * QB, (j + 1) * QB)
         q = q_ref[rows, :] * jnp.asarray(SCALE, BF16)
         qt = q.T
@@ -452,12 +463,12 @@
 
 
 def attend_kernel(bits, parts, chunks, flag_ref, q_ref, kv_ref, kvp_ref, do_ref, gw_ref, gr_ref,
-                  o_ref, dq_ref, dkv_ref, dkvn_ref, outw_ref, outr_ref, *refs):
+                  o_ref, dq_ref, dkv_ref, dkvn_ref, partw_ref, partr_ref, *refs):
     nchunk = len(chunks)
     own, refs = refs[:nchunk], refs[nchunk:]
-    recv = [refs[c * (bits + 1):(c + 1) * (bits + 1)] for c in range(nchunk)]
+    recv = [refs[c * bits:(c + 1) * bits] for c in range(nchunk)]
     (pt, ds, kvt, qm, dom, back, own_sem, send_sem, recv_sem, back_send, back_recv) = refs[
-        nchunk * (bits + 1):]
+        nchunk * bits:]
     red = Halving(bits, parts, chunks, (gw_ref, gr_ref), own, recv, send_sem, recv_sem)
     step = pl.program_id(0)
     steps = dkvn_ref.shape[2] // PAIR
@@ -477,47 +488,69 @@
         red.barrier()
         for c in range(nchunk):
             red.start(c, 0)
-        for c in range(nchunk):
             own_copy(c).start()
 
-    moments = [max(1, steps * m // 8) for m in (1, 4, 6)]
-    moments += [moments[-1]] * (bits - 3)
-    for stage in range(bits):
-        @pl.when(step == moments[stage])
-        def _(stage=stage):
-            for c in range(nchunk):
-                if stage == 0:
-                    own_copy(c).wait()
-                red.add(c, stage)
-                red.start(c, stage + 1)
-
-    @pl.when(step >= 2)
+    moments = {}
+    for c in range(nchunk):
+        times = (2, 6, 11) if c < 2 else (2, 8, 13)
+        for stage in range(bits):
+            at = times[min(stage, 2)] + max(0, stage - 2)
+            moments.setdefault(min(at * steps // 8, 2 * steps - 1), []).append((c, stage))
+
+    def advance(half):
+        for at, work in moments.items():
+            if at % 2 == half:
+                @pl.when(step == at // 2)
+                def _(work=work):
+                    for c, stage in work:
+                        if stage == 0:
+                            own_copy(c).wait()
+                        red.add(c, stage)
+                        if stage + 1 < bits:
+                            red.start(c, stage + 1)
+
+    first, last = red.me_s == 0, red.me_s == parts - 1
+    slot = lax.rem(step, 2)
+
+    @pl.when(jnp.logical_and(step == 0, last))
+    def _():
+        back[1] = jnp.zeros(back.shape[1:], BF16)
+        fills = [pltpu.make_async_copy(back.at[1], dkvn_ref.at[:, :, pl.ds(i * PAIR, PAIR)], back_recv.at[i])
+                 for i in range(steps)]
+        for fill in fills:
+            fill.start()
+        for fill in fills:
+            fill.wait()
+
+    advance(0)
+
+    @pl.when(jnp.logical_and(step >= 2, jnp.logical_not(first)))
     def _():
         back_copy(step - 2).wait_send()
 
     attend_pair(flag_ref, q_ref, kv_ref, kvp_ref, do_ref, o_ref, dq_ref, dkv_ref,
-                back.at[lax.rem(step, 2)], pt, ds, kvt, qm, dom)
-    back_copy(step).start()
+                back.at[slot], pt, ds, kvt, qm, dom, lambda: advance(1))
+
+    @pl.when(jnp.logical_not(first))
+    def _():
+        back_copy(step).start()
 
     @pl.when(step == steps - 1)
     def _():
-        rows = outw_ref.shape[0]
-        width = outr_ref.shape[1]
         for c in range(nchunk):
             mat, col, size, _ = chunks[c]
-            total = red.total(c)
-            if mat == 0:
-                outw_ref[:, col:col + size] = total
-            else:
-                for n in range(size // width):
-                    j = col // width + n
-                    outr_ref[j * rows:(j + 1) * rows, :] = total[:, n * width:(n + 1) * width]
-        for c in range(nchunk):
-            red.wait_sends(c)
-        for i in range(max(0, steps - 2), steps):
-            back_copy(i).wait_send()
-        for i in range(steps):
-            back_copy(i).wait_recv()
+            (partw_ref, partr_ref)[mat][:, :, col:col + size] = recv[c][bits - 1][...]
+            red.wait_sends(c, bits)
+
+        @pl.when(jnp.logical_not(first))
+        def _():
+            for i in range(max(0, steps - 2), steps):
+                back_copy(i).wait_send()
+
+        @pl.when(jnp.logical_not(last))
+        def _():
+            for i in range(steps):
+                back_copy(i).wait_recv()
 
 
 def attend(bits, parts, flag, q, kv, kvp, do, gw, gr):
@@ -535,18 +568,17 @@
     hbm = pl.BlockSpec(memory_space=pl.ANY)
     tok_shape = jax.ShapeDtypeStruct((rows, width), BF16)
     kv_shape = jax.ShapeDtypeStruct((2, rows, width), BF16)
-    fold = hidden // width
-    outw, outr = (take, hidden), (take * fold, width)
+    part = (parts, take, hidden)
     return pl.pallas_call(
         partial(attend_kernel, bits, parts, chunks),
         grid=(steps,),
         out_shape=(tok_shape, tok_shape, kv_shape, kv_shape,
-                   jax.ShapeDtypeStruct(outw, F32), jax.ShapeDtypeStruct(outr, F32)),
+                   jax.ShapeDtypeStruct(part, BF16), jax.ShapeDtypeStruct(part, BF16)),
         in_specs=[pl.BlockSpec(memory_space=pltpu.SMEM), tok, kvs, kvs, tok, hbm, hbm],
-        out_specs=(tok, tok, kvs, hbm, whole(outw), whole(outr)),
+        out_specs=(tok, tok, kvs, hbm, whole(part), whole(part)),
         scratch_shapes=[
             pltpu.VMEM((2,) * (bits - 1) + (parts, take, size), BF16) for _, _, size, _ in chunks
-        ] + halving_scratch(bits, parts, take, chunks) + [
+        ] + halving_scratch(bits, parts, take, chunks, False) + [
             pltpu.VMEM((2, 2 * rows, rows), BF16),
             pltpu.VMEM((2, 2 * rows, rows), BF16),
             pltpu.VMEM((2, PAIR, 2 * rows), BF16),
@@ -566,65 +598,6 @@
     )(flag, q, kv, kvp, do, *shaped)
 
 
-def qkv_back_kernel(x_ref, gain_ref, shift_ref, w_ref, ang_ref, dq_ref, dkv_ref, dkvn_ref,
-                    og_ref, part_ref, dw_ref, db_ref, ig_ref, dgain_ref, dshift_ref,
-                    norm, norm_t, tab, fg):
-    step = pl.program_id(0)
-
-    @pl.when(step == 0)
-    def _():
-        norm_rows(x_ref, gain_ref, shift_ref, norm)
-        norm_t[...] = norm[...].T
-        build_tables(ang_ref, tab)
-        fg[...] = jnp.zeros_like(fg)
-
-    blocks = []
-    for n in range(STEP_PAIRS):
-        mine = slice(n * PAIR, (n + 1) * PAIR)
-        dq = turn(dq_ref[:, mine].astype(F32), tab, -1.0)
-        dk = turn(dkv_ref[0, :, mine].astype(F32) + dkvn_ref[0, :, mine].astype(F32), tab, -1.0)
-        dv = dkv_ref[1, :, mine].astype(F32) + dkvn_ref[1, :, mine].astype(F32)
-        low = low_lanes(dq.shape)
-        dk = pltpu.roll(dk, HEAD_DIM, 1)
-        blocks += [jnp.where(low, dq, dk), jnp.where(low, dv, dq), jnp.where(low, dk, dv)]
-    dm = jnp.concatenate(blocks, axis=1).astype(BF16)
-    db_ref[...] = jnp.sum(dm.astype(F32), axis=0, keepdims=True)
-    dw_ref[...] = dot(norm_t[...], dm).astype(BF16)
-    fg[...] += dot_t(dm, w_ref[...])
-
-    @pl.when(step == pl.num_programs(0) - 1)
-    def _():
-        def emit(rows, part):
-            total = og_ref[rows, :].astype(F32) + part + part_ref[rows, :]
-            ig_ref[rows, :] = total.astype(BF16)
-
-        norm_back(x_ref, gain_ref, fg, dgain_ref, dshift_ref, emit)
-
-
-def qkv_back(x, gain, shift, w, ang, dq, dkv, dkvn, og, part):
-    rows, width = x.shape
-    full, vec = whole((rows, width)), whole((1, width))
-    wide = STEP_PAIRS * PAIR
-    cols = 3 * wide
-    tok = pl.BlockSpec((rows, wide), lambda i: (0, i))
-    kvs = pl.BlockSpec((2, rows, wide), lambda i: (0, 0, i))
-    up, bias = pl.BlockSpec((width, cols), lambda i: (0, i)), pl.BlockSpec((1, cols), lambda i: (0, i))
-    vshape = jax.ShapeDtypeStruct((1, width), F32)
-    return pl.pallas_call(
-        qkv_back_kernel,
-        grid=(width // wide,),
-        out_shape=(jax.ShapeDtypeStruct((width, 3 * width), BF16), jax.ShapeDtypeStruct((1, 3 * width), F32),
-                   jax.ShapeDtypeStruct((rows, width), BF16), vshape, vshape),
-        in_specs=[full, vec, vec, up, whole(ang.shape), tok, kvs, kvs, full, full],
-        out_specs=(up, bias, full, vec, vec),
-        scratch_shapes=[pltpu.VMEM((rows, width), BF16), pltpu.VMEM((width, rows), BF16),
-                        pltpu.VMEM((3, rows, PAIR), F32), pltpu.VMEM((rows, width), F32)],
-        compiler_params=params(),
-        cost_estimate=cost(12 * rows * width * width, 8 * rows * width),
-        name="qkv_back",
-    )(x, gain, shift, w, ang, dq, dkv, dkvn, og, part)
-
-
 def dense_kernel(o_ref, wd_ref, db_ref, rb_ref, mid_ref, x_ref, og_ref, out_ref, dwd_ref, ot):
     @pl.when(pl.program_id(0) == 0)
     def _():
@@ -652,21 +625,64 @@
     )(o, wd, db, rb, mid, x, og)
 
 
-def scatter_kernel(bits, parts, nmat, chunks, vec_sizes, *refs):
-    nvec, nchunk = len(vec_sizes), len(chunks)
-    mats, vecs = refs[:nmat], refs[nmat:nmat + nvec]
-    outs, vec_out = refs[nmat + nvec:2 * nmat + nvec], refs[2 * nmat + nvec]
-    refs = refs[2 * nmat + nvec + 1:]
+def tail_kernel(bits, parts, chunks, x_ref, gain_ref, gain2_ref, norm_t, w_ref, ang_ref, dq_ref, dkv_ref,
+                dkvn_ref, og_ref, sg_ref, dwd_ref, partw_ref, partr_ref, dog_ref, dbe_ref,
+                ig_ref, dw_out, dwd_out, dwe_out, dwr_out, vec_out, *refs):
+    nchunk = len(chunks)
     recv = [refs[c * (bits + 1):(c + 1) * (bits + 1)] for c in range(nchunk)]
-    state, vrecv, send_sem, recv_sem = refs[nchunk * (bits + 1):]
-    red = Halving(bits, parts, chunks, mats, None, recv, send_sem, recv_sem)
-    red.barrier()
-    for c in range(nchunk):
-        red.start(c, 0)
-    at = 0
-    for ref, n in zip(vecs, vec_sizes):
-        state[0, :, at:at + n] = ref[...]
-        at += n
+    (tab, fg, dw, db, dgain, dshift, dgain2, dshift2, zw, zr, state, vrecv, send_sem, recv_sem) = refs[
+        nchunk * (bits + 1):]
+    red = Halving(bits, parts, chunks, (dw, dwd_ref), None, recv, send_sem, recv_sem)
+    step = pl.program_id(0)
+    steps = pl.num_programs(0)
+    width = x_ref.shape[1]
+    nstep = width // (STEP_PAIRS * PAIR)
+    cols = 3 * STEP_PAIRS * PAIR
+
+    def forward(c, stage):
+        red.add(c, stage)
+        red.start(c, stage + 1)
+
+    def z_copies():
+        return [red.copy(nchunk + 1 + m, bits + n, part.at[peer[1]], dst.at[n], peer)
+                for m, (part, dst) in enumerate(((partw_ref, zw), (partr_ref, zr)))
+                for n, peer in enumerate(red.others)]
+
+    @pl.when(step == 0)
+    def _():
+        red.barrier()
+        for copy in z_copies():
+            copy.start()
+        for c in range(nstep, nchunk):
+            red.start(c, 0)
+        build_tables(ang_ref, tab)
+        fg[...] = jnp.zeros_like(fg)
+
+    for c in range(1, nstep):
+        @pl.when(step == c)
+        def _(c=c):
+            red.start(c - 1, 0)
+            if c == 1:
+                for extra in range(nstep, nchunk):
+                    forward(extra, 0)
+            else:
+                forward(c - 2, 0)
+
+    blocks = []
+    for n in range(STEP_PAIRS):
+        mine = slice(n * PAIR, (n + 1) * PAIR)
+        dq = turn(dq_ref[:, mine].astype(F32), tab, -1.0)
+        dk = turn(dkv_ref[0, :, mine].astype(F32) + dkvn_ref[0, :, mine].astype(F32), tab, -1.0)
+        dv = dkv_ref[1, :, mine].astype(F32) + dkvn_ref[1, :, mine].astype(F32)
+        low = low_lanes(dq.shape)
+        dk = pltpu.roll(dk, HEAD_DIM, 1)
+        blocks += [jnp.where(low, dq, dk), jnp.where(low, dv, dq), jnp.where(low, dk, dv)]
+    dm = jnp.concatenate(blocks, axis=1).astype(BF16)
+    at = pl.ds(pl.multiple_of(step * cols, cols), cols)
+    db[:, at] = jnp.sum(dm.astype(F32), axis=0, keepdims=True)
+    dw[(slice(None),) * (bits + 2) + (at,)] = dot(norm_t[...], dm).reshape(
+        dw.shape[:-1] + (cols,)).astype(BF16)
+    fg[...] += dot_t(dm, w_ref[...])
 
     def vec_copies(stage):
         if stage < bits:
@@ -691,55 +707,124 @@
         else:
             vec_out[...] = total
 
-    vec_start(0)
-    for stage in range(bits + 1):
+    @pl.when(step == steps - 1)
+    def _():
+        red.start(nstep - 1, 0)
+        forward(nstep - 2, 0)
+
+        def emit(rows, part):
+            ig_ref[rows, :] = (og_ref[rows, :].astype(F32) + part).astype(BF16)
+
+        forward(nstep - 1, 0)
+        norm_back(x_ref, (gain_ref, gain2_ref), (fg, sg_ref), (dgain, dgain2), (dshift, dshift2), emit)
+        begin = 0
+        for ref in (dgain, dshift, db, dog_ref, dgain2, dshift2, dbe_ref):
+            state[0, :, begin:begin + ref.shape[1]] = ref[...]
+            begin += ref.shape[1]
+        vec_start(0)
+        order = list(range(nstep, nchunk)) + list(range(nstep))
+        for stage in range(1, bits):
+            for c in order:
+                forward(c, stage)
+            vec_add(stage - 1)
+        copies = z_copies()
+        for m, (part, got, out) in enumerate(((partw_ref, zw, dwe_out), (partr_ref, zr, dwr_out))):
+            total = part[red.me_s].astype(F32)
+            for n in range(parts - 1):
+                copies[m * (parts - 1) + n].wait_recv()
+                total = total + got[n].astype(F32)
+            if m == 0:
+                out[...] = total
+            else:
+                take = total.shape[0]
+                for j in range(total.shape[1] // width):
+                    out[j * take:(j + 1) * take, :] = total[:, j * width:(j + 1) * width]
+        vec_add(bits - 1)
+        for c in order:
+            mat, col, size, _ = chunks[c]
+            (dw_out, dwd_out)[mat][:, col:col + size] = red.total(c)
+        vec_add(bits)
         for c in range(nchunk):
-            if stage < bits:
-                red.add(c, stage)
-                red.start(c, stage + 1)
-            else:
-                mat, col, size, _ = chunks[c]
-                outs[mat][:, col:col + size] = red.total(c)
-        vec_add(stage)
-    for c in range(nchunk):
-        red.wait_sends(c)
-    for stage in range(bits + 1):
-        for copy in vec_copies(stage):
+            red.wait_sends(c, bits + 1)
+        for copy in copies:
             copy.wait_send()
-
-
-def scatter(bits, parts, mats, vecs):
-    shards = parts << bits
-    rows = mats[0].shape[0] // shards
-    widths = [m.shape[1] for m in mats]
-    shaped = [m.reshape((2,) * bits + (parts, rows, m.shape[1])) for m in mats]
+        for stage in range(bits + 1):
+            for copy in vec_copies(stage):
+                copy.wait_send()
+
+
+def tail(bits, parts, x, gain, gain2, norm_t, w, ang, dq, dkv, dkvn, og, sg, dwd, partw, partr, dog, dbe):
+    rows, width = x.shape
+    full, vec = whole((rows, width)), whole((1, width))
+    wide = STEP_PAIRS * PAIR
+    cols = 3 * wide
+    nstep = width // wide
+    hidden = dbe.shape[1]
+    take = width // (parts << bits)
+    total = 5 * width + 3 * width + hidden
+    npeer = bits + parts - 1
+    lead = (2,) * bits + (parts, take)
     plain, other = halving_orders(bits)
-    chunks = []
-    for m, w in enumerate(widths):
-        size = w // 4 if w > 2048 else w // 2
-        for n in range(w // size):
-            chunks.append((m, n * size, size, other if n % 2 else plain))
-    vec_sizes = [v.shape[1] for v in vecs]
-    total = sum(vec_sizes)
-    npeer = bits + parts - 1
-    scratch = halving_scratch(bits, parts, rows, chunks) + [
-        pltpu.VMEM((bits + 1, 1, total), F32),
-        pltpu.VMEM((npeer, 1, total), F32),
-        pltpu.SemaphoreType.DMA((len(chunks) + 1, npeer)),
-        pltpu.SemaphoreType.DMA((len(chunks) + 1, npeer)),
-    ]
-    vmem = pl.BlockSpec(memory_space=pltpu.VMEM)
+    chunks = [(0, n * cols, cols, other if n % 2 else plain) for n in range(nstep)]
+    chunks += [(1, n * (width // 2), width // 2, other if n % 2 else plain) for n in range(2)]
+    tok = pl.BlockSpec((rows, wide), lambda i: (0, i))
+    kvs = pl.BlockSpec((2, rows, wide), lambda i: (0, 0, i))
+    up = pl.BlockSpec((width, cols), lambda i: (0, i))
+    dwd = dwd.reshape(lead + (width,))
+    outs = [((rows, width), BF16), ((take, 3 * width), F32), ((take, width), F32), ((take, hidden), F32),
+            ((take * (hidden // width), width), F32), ((1, total), F32)]
+    row_vec = pltpu.VMEM((1, width), F32)
+    nsem = (len(chunks) + 3, npeer)
     return pl.pallas_call(
-        partial(scatter_kernel, bits, parts, len(mats), chunks, vec_sizes),
-        out_shape=tuple(jax.ShapeDtypeStruct((rows, w), F32) for w in widths)
-        + (jax.ShapeDtypeStruct((1, total), F32),),
-        in_specs=[vmem] * (len(mats) + len(vecs)),
-        out_specs=tuple([vmem] * (len(mats) + 1)),
-        scratch_shapes=scratch,
+        partial(tail_kernel, bits, parts, chunks),
+        grid=(nstep,),
+        out_shape=tuple(jax.ShapeDtypeStruct(s, d) for s, d in outs),
+        in_specs=[full, vec, vec, whole(norm_t.shape), up, whole(ang.shape), tok, kvs, kvs, full, full,
+                  whole(dwd.shape), whole(partw.shape), whole(partr.shape), vec, whole(dbe.shape)],
+        out_specs=tuple(whole(s) for s, _ in outs),
+        scratch_shapes=halving_scratch(bits, parts, take, chunks, True) + [
+            pltpu.VMEM((3, rows, PAIR), F32), pltpu.VMEM((rows, width), F32),
+            pltpu.VMEM(lead + (3 * width,), BF16), pltpu.VMEM((1, 3 * width), F32),
+            row_vec, row_vec, row_vec, row_vec,
+            pltpu.VMEM((parts - 1, take, hidden), BF16), pltpu.VMEM((parts - 1, take, hidden), BF16),
+            pltpu.VMEM((bits + 1, 1, total), F32), pltpu.VMEM((npeer, 1, total), F32),
+            pltpu.SemaphoreType.DMA(nsem), pltpu.SemaphoreType.DMA(nsem),
+        ],
         compiler_params=pltpu.CompilerParams(
-            vmem_limit_bytes=VMEM_LIMIT, collective_id=0, has_side_effects=True),
-        name="scatter",
-    )(*shaped, *vecs)
+            vmem_limit_bytes=63 << 20, collective_id=0, has_side_effects=True),
+        cost_estimate=cost(12 * rows * width * width, 8 * rows * width),
+        name="tail",
+    )(x, gain, gain2, norm_t, w, ang, dq, dkv, dkvn, og, sg, dwd, partw, partr, dog, dbe)
+
+
+def finish_kernel(sizes, index_ref, ig_ref, dw_ref, dwd_ref, dwe_ref, dwr_ref, vec_ref,
+                  ig_out, dw_out, dwd_out, dwe_out, dwr_out, *outs):
+    for src, dst in ((ig_ref, ig_out), (dw_ref, dw_out), (dwd_ref, dwd_out), (dwe_ref, dwe_out),
+                     (dwr_ref, dwr_out)):
+        dst[...] = src[...]
+
+    @pl.when(pl.program_id(0) == 0)
+    def _():
+        at = 0
+        for size, out in zip(sizes, outs):
+            own = out.shape[1]
+            row = jnp.broadcast_to(vec_ref[:, at:at + size], (8, size))
+            out[...] = pltpu.roll(row, lax.rem(size - index_ref[0] * own, size), 1)[:1, :own]
+            at += size
+
+
+def finish(index, ndev, sizes, ig, dw, dwd, dwe, dwr, vec):
+    mats = (ig, dw, dwd, dwe, dwr)
+    return pl.pallas_call(
+        partial(finish_kernel, sizes),
+        out_shape=tuple(jax.ShapeDtypeStruct(m.shape, m.dtype) for m in mats)
+        + tuple(jax.ShapeDtypeStruct((1, n // ndev), F32) for n in sizes),
+        grid=(1,),
+        in_specs=[pl.BlockSpec(memory_space=pltpu.SMEM)] + [whole(m.shape) for m in mats] + [whole(vec.shape)],
+        out_specs=tuple([whole(m.shape) for m in mats] + [whole((1, n // ndev)) for n in sizes]),
+        compiler_params=params(),
+        name="finish",
+    )(index, *mats, vec)
 
 
 def body(
@@ -779,26 +864,23 @@
     batch_parts = lax.axis_size("batch")
     ndev = batch_parts * seq_parts
     bits = batch_parts.bit_length() - 1
-    q, kv, do = project(tokens, ag, ash, qkv_weight, row(qkv_bias), ang, out_grad, dense_weight)
+    q, kv, do, n1t, n2, n2t = project(
+        tokens, ag, ash, mg, msh, qkv_weight, row(qkv_bias), ang, out_grad, dense_weight)
     kvp = lax.ppermute(kv, "seq", onward)
     mid, slope, dwr, dog = mlp_fwd(
-        ndev, tokens, mg, msh, expand_weight, row(expand_bias), reduce_weight, out_grad)
-    part, dwe, dbe, dmg, dms = mlp_back(
-        tokens, mg, msh, expand_weight, reduce_weight, out_grad, slope)
-
-    o, dq, dkv, dkvn, dwe, dwr = attend(bits, seq_parts, flag, q, kv, kvp, do, dwe, dwr)
+        ndev, n2, expand_weight, row(expand_bias), reduce_weight, out_grad)
+    sg, dwe, dbe = mlp_back(n2t, expand_weight, reduce_weight, out_grad, slope)
+
+    o, dq, dkv, dkvn, partw, partr = attend(bits, seq_parts, flag, q, kv, kvp, do, dwe, dwr)
     layer_out, dwd = dense(o, dense_weight, row(dense_bias), row(reduce_bias), mid, tokens, out_grad)
-    dw, db, input_grad, dag, das = qkv_back(
-        tokens, ag, ash, qkv_weight, ang, dq, dkv, dkvn, out_grad, part)
-    vecs = [dag, das, db, dog, dmg, dms, dbe]
-    dw, dwd, vsum = scatter(bits, seq_parts, [dw, dwd], vecs)
+    input_grad, dw, dwd, dwe, dwr, vsum = tail(
+        bits, seq_parts, tokens, ag, mg, n1t, qkv_weight, ang, dq, dkv, dkvn, out_grad, sg, dwd,
+        partw, partr, dog, dbe)
     index = lax.axis_index("batch") * seq_parts + place
-    pieces, at = [], 0
-    for size in (width, width, 3 * width, width, width, width, dbe.shape[1]):
-        own = size // ndev
-        pieces.append(lax.dynamic_slice(vsum, (0, at + index * own), (1, own)).reshape(own))
-        at += size
-    dag, das, dqb, dog, dmg, dms, dbe = pieces
+    sizes = (width, width, 3 * width, width, width, width, dbe.shape[1])
+    input_grad, dw, dwd, dwe, dwr, *vectors = finish(
+        index.astype(jnp.int32).reshape(1), ndev, sizes, input_grad, dw, dwd, dwe, dwr, vsum)
+    dag, das, dqb, dog, dmg, dms, dbe = [v.reshape(-1) for v in vectors]
     return (
         layer_out,
         input_grad,

time: 434 us -> 388 us (0.89)
  Pallas kernels: 409 us -> 371 us
  local copies, waits for them, and re-layouts: 9.17 us -> 1.17 us
    pallas_call x2, Pallas kernels: 108 us -> 89.8 us  [the longest x1 85.8 us: tail(): pl.pallas_call(partial(tail_kernel, bits, parts, chunks), grid=(nstep,),...]
    pallas_call x1, Pallas kernels: 164 us -> 152 us  [attend(): pl.pallas_call(partial(attend_kernel, bits, parts, chunks), grid=(steps,)...]
    pallas_call x1, Pallas kernels: 55.1 us -> 47.9 us  [mlp_back(): pl.pallas_call(mlp_back_kernel, grid=(hidden // FB,), out_shape=(jax.Shap...]
where the time goes in v2:
time: 388 us; the launch traced here: 384 us
  Pallas kernels  371 us (96%)
  starting transfers between devices  7.34 us (2%)
    pallas_call x1, Pallas kernels, attend(): pl.pallas_call(partial(attend_kernel, bits, parts, chunks), grid=(steps,)...  152 us
    pallas_call x1, Pallas kernels, tail(): pl.pallas_call(partial(tail_kernel, bits, parts, chunks), grid=(nstep,),...  85.8 us
    pallas_call x1, Pallas kernels, mlp_fwd(): pl.pallas_call(partial(mlp_fwd_kernel, out_rows // ndev), grid=(hidden //...  49.2 us
    pallas_call x1, Pallas kernels, mlp_back(): pl.pallas_call(mlp_back_kernel, grid=(hidden // FB,), out_shape=(jax.Shap...  47.9 us
    pallas_call x1, Pallas kernels, project(): pl.pallas_call(project_kernel, grid=(width // wide,), out_shape=(jax.Shap...  21.2 us
    pallas_call x1, Pallas kernels, dense(): pl.pallas_call(dense_kernel, grid=(width // blk,), out_shape=(jax.ShapeDt...  10.7 us
  transfers between devices with their start and end apart: 1, of which 0 were waited for; matrix products, arithmetic and copies ran while one was open for 0% of the time, Pallas kernels for 25%

profile of v2, /device:TPU:0, one launch (start us, length us, event | category | flops | bytes accessed | tf_op | source)
XLA Modules:
  0.0 384.0 jit_solution(12634013363684751659)
XLA Ops:
  0.7 0.8 reduce-window.9
  1.5 1.3 fusion
  3.5 0.2 multiply_cosine_fusion
  3.7 0.6 pad_maximum_fusion.ang_ref
  4.3 21.2 %project.1 = (bf16[1024,1024]{1,0:T(8,128)(2,1)}, bf16[2,1024,1024]{2,1,0:T(8,128)(2,1)}, bf16[1024,1024]{1,0:T(8,128)(2,1)}, bf16[1024,1024]{1,0:T(8,128)(2,1)}...) custom-call(bf16[1024,1024]{1,0:T(8,128)(2,1)} %x_ref.5, f32[1,1024]{1,0:T(1,128)} %bitcast.34, ...), custom_call_target="tpu_custom_call" | custom-call | flops 8589934592 | bytes 25165824 | tf_op jit(solution)/shard_map/project/pallas_call | solution.py:155
  25.5 7.3 %collective-permute-start = (bf16[2,1024,1024]{2,1,0:T(8,128)(2,1)}, bf16[2,1024,1024]{2,1,0:T(8,128)(2,1)}, u32[]{:S(2)}, u32[]{:S(2)}) collective-permute-start(bf16[2,1024,1024]{2,1,0:T(8,128)(2,1)} %get-tuple-element.54.kv_ref), channel_id=1, source_target_pairs={{0,1},{1,2},{2,3},{4,5},{5,6},{6,7},{8,9},{9,10},{10,11},{12,13},{... | collective-permute-start | bytes 12582920 | tf_op jit(solution)/shard_map/ppermute | solution.py:869
  32.8 49.2 %mlp_fwd.1 = (f32[1024,1024]{1,0:T(8,128)}, bf16[1024,4096]{1,0:T(8,128)(2,1)}, bf16[1024,4096]{1,0:T(8,128)(2,1)}, f32[1,1024]{1,0:T(1,128)}) custom-call(bf16[1024,1024]{1,0:T(8,128)(2,1)} %get-tuple-element.57.norm, bf16[1024,4096]{1,0:T(8,128)(2,1)} %we_ref.3, f32[1,4096]{1,0:T(1,128)} %bitcast.28, bf16[4096,1024]{1,0:T(8,128)(2,1)} %wr_ref.3, ...), custom_call_target="tpu_custom_call" | custom-call | flops 25769803776 | bytes 33554432 | tf_op jit(solution)/shard_map/mlp_fwd/pallas_call | solution.py:250
  82.0 47.9 %mlp_back.1 = (f32[1024,1024]{1,0:T(8,128)}, bf16[1024,4096]{1,0:T(8,128)(2,1)}, f32[1,4096]{1,0:T(1,128)}) custom-call(bf16[1024,1024]{1,0:T(8,128)(2,1)} %get-tuple-element.56.norm_t, bf16[1024,4096]{1,0:T(8,128)(2,1)} %we_ref.3, bf16[4096,1024]{1,0:T(8,128)(2,1)} %wr_ref.3, bf16[1024,1024]{1,0:T(8,128)(2,1)} %og_ref.9, ...), custom_call_target="tpu_custom_call" | custom-call | flops 25769803776 | bytes 33554432 | tf_op jit(solution)/shard_map/mlp_back/pallas_call | solution.py:267
  129.9 0.0 collective-permute-done.kvp_ref
  129.9 152.2 %attend.1 = (bf16[1024,1024]{1,0:T(8,128)(2,1)}, bf16[1024,1024]{1,0:T(8,128)(2,1)}, bf16[2,1024,1024]{2,1,0:T(8,128)(2,1)}, bf16[2,1024,1024]{2,1,0:T(8,128)(2,...) custom-call(s32[1]{0:T(128)} %bitcast.3.flag_ref, bf16[1024,1024]{1,0:T(8,128)(2,1)} %get-tuple-element.53.q_ref, ...), custom_call_target="tpu_custom_call" | custom-call | flops 64424509440 | bytes 20971520 | tf_op jit(solution)/shard_map/attend/pallas_call | solution.py:572
  282.1 10.7 %dense.1 = (bf16[1024,1024]{1,0:T(8,128)(2,1)}, bf16[1024,1024]{1,0:T(8,128)(2,1)}) custom-call(bf16[1024,1024]{1,0:T(8,128)(2,1)} %get-tuple-element.61.o_ref, bf16[1024,1024]{1,0:T(8,128)(2,1)} %wd_ref.3, f32[1,1024]{1,0:T(1,128)} %bitcast.32, f32[1,1024]{1,0:T(1,128)} %bitcast.33, f32[1024,1024]{1,0:T(8,128)} %get-tuple-element.62.mid_ref, ...), custom_call_target="tpu_custom_call" | custom-call | flops 4294967296 | bytes 12582912 | tf_op jit(solution)/shard_map/dense/pallas_call | solution.py:615
  292.9 85.8 %tail.1 = (bf16[1024,1024]{1,0:T(8,128)(2,1)}, f32[32,3072]{1,0:T(8,128)}, f32[32,1024]{1,0:T(8,128)}, f32[32,4096]{1,0:T(8,128)}, f32[128,1024]{1,0:T(8,128)}, /*index=5*/f32[1,12288]{1,0:T(1,128)}) custom-call(bf16[1024,1024]{1,0:T(8,128)(2,1)} %x_ref.5, f32[1,1024]{1,0:T(1,128)} %bitcast.35, f32[1,1024]{1,0:T(1,128)} %bitcast.37, ...), custom_call_target="tpu_custom_call" | custom-call | flops 12884901888 | bytes 8388608 | tf_op jit(solution)/shard_map/tail/pallas_call | solution.py:778
  378.6 4.0 %finish.1 = (bf16[1024,1024]{1,0:T(8,128)(2,1)}, f32[32,3072]{1,0:T(8,128)}, f32[32,1024]{1,0:T(8,128)}, f32[32,4096]{1,0:T(8,128)}, f32[128,1024]{1,0:T(8,128)}...) custom-call(s32[1]{0:T(128)} %bitcast.14.index_ref, ...), custom_call_target="tpu_custom_call" | custom-call | tf_op jit(solution)/shard_map/finish/pallas_call | solution.py:818
  382.6 1.2 copy.30
  (2 shorter events, 0.0 us)
Async XLA Ops:
  25.5 104.5 %collective-permute-start = (bf16[2,1024,1024]{2,1,0:T(8,128)(2,1)}, bf16[2,1024,1024]{2,1,0:T(8,128)(2,1)}, u32[]{:S(2)}, u32[]{:S(2)}) collective-permute-start(bf16[2,1024,1024]{2,1,0:T(8,128)(2,1)} %get-tuple-element.54.kv_ref), channel_id=1, source_target_pairs={{0,1},{1,2},{2,3},{4,5},{5,6},{6,7},{8,9},{9,10},{10,11},{12,13},{... | collective-permute-start | bytes 12582920 | tf_op jit(solution)/shard_map/ppermute | solution.py:869

commit v3 on v2

--- a/solution.py
+++ b/solution.py
@@ -67,9 +67,10 @@
     lax.fori_loop(0, x_ref.shape[0] // ROWS, step, 0)
 
 
-def norm_back(x_ref, gains, grads, gain_grads, shift_grads, emit):
-    for ref in gain_grads + shift_grads:
-        ref[...] = jnp.zeros_like(ref)
+def norm_back(x_ref, gains, grads, gain_grads, shift_grads, emit, begin, end):
+    if begin == 0:
+        for ref in gain_grads + shift_grads:
+            ref[...] = jnp.zeros_like(ref)
 
     def step(i, carry):
         rows = row_block(i)
@@ -85,7 +86,7 @@
         emit(rows, rstd * (scaled - mean_s - xn * mean_sx))
         return carry
 
-    lax.fori_loop(0, x_ref.shape[0] // ROWS, step, 0)
+    lax.fori_loop(begin, end, step, 0)
 
 
 def build_tables(angle_ref, tab_ref):
@@ -113,7 +114,7 @@
 
 
 def project_kernel(x_ref, gain_ref, shift_ref, gain2_ref, shift2_ref, w_ref, b_ref, ang_ref, og_ref,
-                   wd_ref, q_ref, kv_ref, do_ref, n1t_ref, n2_ref, n2t_ref,
+                   wd_ref, q_ref, kv_ref, kvh_ref, do_ref, n1t_ref, n2_ref, n2t_ref,
                    norm, n1t, n2, n2t, tab, sem):
     saves = [pltpu.make_async_copy(src, dst, sem.at[n]) for n, (src, dst) in enumerate(
         ((n1t, n1t_ref), (n2, n2_ref), (n2t, n2t_ref)))]
@@ -142,6 +143,10 @@
         kv_ref[1, :, mine] = v.astype(BF16)
     do_ref[...] = dot_t(og_ref[...], wd_ref[...]).astype(BF16)
 
+    @pl.when(pl.program_id(0) < pl.num_programs(0) // 2)
+    def _():
+        kvh_ref[...] = kv_ref[...]
+
     @pl.when(pl.program_id(0) == pl.num_programs(0) - 1)
     def _():
         for save in saves:
@@ -158,6 +163,7 @@
         out_shape=(
             jax.ShapeDtypeStruct((rows, width), BF16),
             jax.ShapeDtypeStruct((2, rows, width), BF16),
+            jax.ShapeDtypeStruct((2, rows, width // 2), BF16),
             jax.ShapeDtypeStruct((rows, width), BF16),
             jax.ShapeDtypeStruct((width, rows), BF16),
             jax.ShapeDtypeStruct((rows, width), BF16),
@@ -170,7 +176,8 @@
             whole(ang.shape), whole((rows, width)),
             pl.BlockSpec((wide, width), lambda i: (i, 0)),
         ],
-        out_specs=(tok, pl.BlockSpec((2, rows, wide), lambda i: (0, 0, i)), tok,
+        out_specs=(tok, pl.BlockSpec((2, rows, wide), lambda i: (0, 0, i)),
+                   pl.BlockSpec((2, rows, wide), lambda i: (0, 0, jnp.minimum(i, width // wide // 2 - 1))), tok,
                    *[pl.BlockSpec(memory_space=pl.ANY)] * 3),
         scratch_shapes=[pltpu.VMEM((rows, width), BF16), pltpu.VMEM((width, rows), BF16),
                         pltpu.VMEM((rows, width), BF16), pltpu.VMEM((width, rows), BF16),
@@ -374,12 +381,12 @@
     return plain, other
 
 
-def halving_scratch(bits, parts, rows, chunks, last):
+def halving_scratch(bits, parts, rows, chunks, ends):
     scratch = []
-    for _, _, size, _ in chunks:
+    for (_, _, size, _), end in zip(chunks, ends):
         for stage in range(bits):
             scratch.append(pltpu.VMEM((2,) * (bits - 1 - stage) + (parts, rows, size), BF16))
-        if last:
+        if end:
             scratch.append(pltpu.VMEM((parts - 1, rows, size), BF16))
     return scratch
 
@@ -462,13 +469,22 @@
         ref[1, i * QB:(i + 1) * QB, :] = dv.astype(BF16)
 
 
-def attend_kernel(bits, parts, chunks, flag_ref, q_ref, kv_ref, kvp_ref, do_ref, gw_ref, gr_ref,
-                  o_ref, dq_ref, dkv_ref, dkvn_ref, partw_ref, partr_ref, *refs):
+def fold_rows(out_ref, total):
+    take, width = total.shape[0], out_ref.shape[1]
+    for j in range(total.shape[1] // width):
+        out_ref[j * take:(j + 1) * take, :] = total[:, j * width:(j + 1) * width]
+
+
+def attend_kernel(bits, parts, chunks, ends, flag_ref, q_ref, kv_ref, kv_hbm, kvp_hbm, do_ref, gw_ref, gr_ref,
+                  o_ref, dq_ref, dkv_ref, dkvn_ref, partw_ref, partr_ref, totw_ref, totr_ref, *refs):
     nchunk = len(chunks)
     own, refs = refs[:nchunk], refs[nchunk:]
-    recv = [refs[c * bits:(c + 1) * bits] for c in range(nchunk)]
-    (pt, ds, kvt, qm, dom, back, own_sem, send_sem, recv_sem, back_send, back_recv) = refs[
-        nchunk * bits:]
+    recv = []
+    for end in ends:
+        recv.append(refs[:bits + end])
+        refs = refs[bits + end:]
+    (pt, ds, kvt, qm, dom, back, kvp, own_sem, send_sem, recv_sem, back_send, back_recv,
+     kv_load, kv_send, kv_recv) = refs
     red = Halving(bits, parts, chunks, (gw_ref, gr_ref), own, recv, send_sem, recv_sem)
     step = pl.program_id(0)
     steps = dkvn_ref.shape[2] // PAIR
@@ -483,16 +499,42 @@
             send_sem=back_send.at[i], recv_sem=back_recv.at[i],
             device_id=red.others[parts - 2], device_id_type=MESH)
 
+    first, last = red.me_s == 0, red.me_s == parts - 1
+    half_steps = steps // 2
+
+    def pair_cols(i):
+        return pl.ds(pl.multiple_of(i * PAIR, PAIR), PAIR)
+
+    def load_copy(i):
+        return pltpu.make_async_copy(kvp_hbm.at[:, :, pair_cols(i)], kvp.at[i], kv_load.at[i])
+
+    def onward_copy(i):
+        return pltpu.make_async_remote_copy(
+            src_ref=kv_hbm.at[:, :, pair_cols(i)], dst_ref=kvp.at[i],
+            send_sem=kv_send.at[i - half_steps], recv_sem=kv_recv.at[i - half_steps],
+            device_id=red.others[0], device_id_type=MESH)
+
     @pl.when(step == 0)
     def _():
         red.barrier()
+        for i in range(half_steps):
+            load_copy(i).start()
         for c in range(nchunk):
             red.start(c, 0)
             own_copy(c).start()
 
+    @pl.when(jnp.logical_and(step == 0, jnp.logical_not(last)))
+    def _():
+        for i in range(half_steps, steps):
+            onward_copy(i).start()
+
+    @pl.when(jnp.logical_and(step == 0, first))
+    def _():
+        kvp[half_steps:] = jnp.zeros((steps - half_steps,) + kvp.shape[1:], BF16)
+
     moments = {}
     for c in range(nchunk):
-        times = (2, 6, 11) if c < 2 else (2, 8, 13)
+        times = (2, 7, 11) if ends[c] else (2, 8, 13)
         for stage in range(bits):
             at = times[min(stage, 2)] + max(0, stage - 2)
             moments.setdefault(min(at * steps // 8, 2 * steps - 1), []).append((c, stage))
@@ -506,10 +548,9 @@
                         if stage == 0:
                             own_copy(c).wait()
                         red.add(c, stage)
-                        if stage + 1 < bits:
+                        if stage + 1 < bits + ends[c]:
                             red.start(c, stage + 1)
 
-    first, last = red.me_s == 0, red.me_s == parts - 1
     slot = lax.rem(step, 2)
 
     @pl.when(jnp.logical_and(step == 0, last))
@@ -528,7 +569,15 @@
     def _():
         back_copy(step - 2).wait_send()
 
-    attend_pair(flag_ref, q_ref, kv_ref, kvp_ref, do_ref, o_ref, dq_ref, dkv_ref,
+    @pl.when(step < half_steps)
+    def _():
+        load_copy(step).wait()
+
+    @pl.when(jnp.logical_and(step >= half_steps, jnp.logical_not(first)))
+    def _():
+        onward_copy(step).wait_recv()
+
+    attend_pair(flag_ref, q_ref, kv_ref, kvp.at[step], do_ref, o_ref, dq_ref, dkv_ref,
                 back.at[slot], pt, ds, kvt, qm, dom, lambda: advance(1))
 
     @pl.when(jnp.logical_not(first))
@@ -539,8 +588,20 @@
     def _():
         for c in range(nchunk):
             mat, col, size, _ = chunks[c]
-            (partw_ref, partr_ref)[mat][:, :, col:col + size] = recv[c][bits - 1][...]
-            red.wait_sends(c, bits)
+            if not ends[c]:
+                (partw_ref, partr_ref)[mat][...] = recv[c][bits - 1][...]
+            red.wait_sends(c, bits + ends[c])
+        for c in range(nchunk):
+            mat, col, size, _ = chunks[c]
+            if ends[c] and mat == 0:
+                totw_ref[...] = red.total(c)
+            elif ends[c]:
+                fold_rows(totr_ref, red.total(c))
+
+        @pl.when(jnp.logical_not(last))
+        def _():
+            for i in range(half_steps, steps):
+                onward_copy(i).wait_send()
 
         @pl.when(jnp.logical_not(first))
         def _():
@@ -556,9 +617,9 @@
 def attend(bits, parts, flag, q, kv, kvp, do, gw, gr):
     rows, width = q.shape
     steps = width // PAIR
-    hidden = gw.shape[1]
+    hidden = gr.shape[1]
     take = gw.shape[0] // (parts << bits)
-    shaped = [g.reshape((2,) * bits + (parts, take, hidden)) for g in (gw, gr)]
+    shaped = [g.reshape((2,) * bits + (parts, take, g.shape[1])) for g in (gw, gr)]
     plain, other = halving_orders(bits)
     chunks = [(0, 0, hidden // 2, plain), (1, 0, hidden // 2, other),
               (0, hidden // 2, hidden // 2, plain), (1, hidden // 2, hidden // 2, other)]
@@ -568,34 +629,41 @@
     hbm = pl.BlockSpec(memory_space=pl.ANY)
     tok_shape = jax.ShapeDtypeStruct((rows, width), BF16)
     kv_shape = jax.ShapeDtypeStruct((2, rows, width), BF16)
-    part = (parts, take, hidden)
+    ends = (1, 1, 0, 0)
+    part = (parts, take, hidden // 2)
+    totw, totr = (take, hidden // 2), (take * hidden // 2 // width, width)
     return pl.pallas_call(
-        partial(attend_kernel, bits, parts, chunks),
+        partial(attend_kernel, bits, parts, chunks, ends),
         grid=(steps,),
         out_shape=(tok_shape, tok_shape, kv_shape, kv_shape,
-                   jax.ShapeDtypeStruct(part, BF16), jax.ShapeDtypeStruct(part, BF16)),
-        in_specs=[pl.BlockSpec(memory_space=pltpu.SMEM), tok, kvs, kvs, tok, hbm, hbm],
-        out_specs=(tok, tok, kvs, hbm, whole(part), whole(part)),
+                   jax.ShapeDtypeStruct(part, BF16), jax.ShapeDtypeStruct(part, BF16),
+                   jax.ShapeDtypeStruct(totw, F32), jax.ShapeDtypeStruct(totr, F32)),
+        in_specs=[pl.BlockSpec(memory_space=pltpu.SMEM), tok, kvs, hbm, hbm, tok, hbm, hbm],
+        out_specs=(tok, tok, kvs, hbm, whole(part), whole(part), whole(totw), whole(totr)),
         scratch_shapes=[
             pltpu.VMEM((2,) * (bits - 1) + (parts, take, size), BF16) for _, _, size, _ in chunks
-        ] + halving_scratch(bits, parts, take, chunks, False) + [
+        ] + halving_scratch(bits, parts, take, chunks, ends) + [
             pltpu.VMEM((2, 2 * rows, rows), BF16),
             pltpu.VMEM((2, 2 * rows, rows), BF16),
             pltpu.VMEM((2, PAIR, 2 * rows), BF16),
             pltpu.VMEM((2, rows, PAIR), BF16),
             pltpu.VMEM((2, rows, PAIR), BF16),
             pltpu.VMEM((2, 2, rows, PAIR), BF16),
+            pltpu.VMEM((steps, 2, rows, PAIR), BF16),
             pltpu.SemaphoreType.DMA((len(chunks),)),
             pltpu.SemaphoreType.DMA((len(chunks), npeer)),
             pltpu.SemaphoreType.DMA((len(chunks), npeer)),
             pltpu.SemaphoreType.DMA((steps,)),
             pltpu.SemaphoreType.DMA((steps,)),
+            pltpu.SemaphoreType.DMA((steps // 2,)),
+            pltpu.SemaphoreType.DMA((steps - steps // 2,)),
+            pltpu.SemaphoreType.DMA((steps - steps // 2,)),
         ],
         compiler_params=pltpu.CompilerParams(
             vmem_limit_bytes=63 << 20, collective_id=1, has_side_effects=True),
         cost_estimate=cost(60 * rows * rows * width, 20 * rows * width),
         name="attend",
-    )(flag, q, kv, kvp, do, *shaped)
+    )(flag, q, kv, kv, kvp, do, *shaped)
 
 
 def dense_kernel(o_ref, wd_ref, db_ref, rb_ref, mid_ref, x_ref, og_ref, out_ref, dwd_ref, ot):
@@ -639,9 +707,13 @@
     nstep = width // (STEP_PAIRS * PAIR)
     cols = 3 * STEP_PAIRS * PAIR
 
+    done = set()
+
     def forward(c, stage):
-        red.add(c, stage)
-        red.start(c, stage + 1)
+        if (c, stage) not in done:
+            done.add((c, stage))
+            red.add(c, stage)
+            red.start(c, stage + 1)
 
     def z_copies():
         return [red.copy(nchunk + 1 + m, bits + n, part.at[peer[1]], dst.at[n], peer)
@@ -667,6 +739,9 @@
                     forward(extra, 0)
             else:
                 forward(c - 2, 0)
+            if c == nstep - 1:
+                for extra in range(nstep, nchunk):
+                    forward(extra, 1)
 
     blocks = []
     for n in range(STEP_PAIRS):
@@ -716,7 +791,14 @@
             ig_ref[rows, :] = (og_ref[rows, :].astype(F32) + part).astype(BF16)
 
         forward(nstep - 1, 0)
-        norm_back(x_ref, (gain_ref, gain2_ref), (fg, sg_ref), (dgain, dgain2), (dshift, dshift2), emit)
+        forward(0, 1)
+        norm_args = (x_ref, (gain_ref, gain2_ref), (fg, sg_ref), (dgain, dgain2), (dshift, dshift2), emit)
+        row_blocks = x_ref.shape[0] // ROWS
+        norm_back(*norm_args, 0, row_blocks // 2)
+        forward(1, 1)
+        for extra in range(nstep, nchunk):
+            forward(extra, 2)
+        norm_back(*norm_args, row_blocks // 2, row_blocks)
         begin = 0
         for ref in (dgain, dshift, db, dog_ref, dgain2, dshift2, dbe_ref):
             state[0, :, begin:begin + ref.shape[1]] = ref[...]
@@ -736,9 +818,7 @@
             if m == 0:
                 out[...] = total
             else:
-                take = total.shape[0]
-                for j in range(total.shape[1] // width):
-                    out[j * take:(j + 1) * take, :] = total[:, j * width:(j + 1) * width]
+                fold_rows(out, total)
         vec_add(bits - 1)
         for c in order:
             mat, col, size, _ = chunks[c]
@@ -759,7 +839,7 @@
     wide = STEP_PAIRS * PAIR
     cols = 3 * wide
     nstep = width // wide
-    hidden = dbe.shape[1]
+    hidden, part = dbe.shape[1], partw.shape[2]
     take = width // (parts << bits)
     total = 5 * width + 3 * width + hidden
     npeer = bits + parts - 1
@@ -771,8 +851,8 @@
     kvs = pl.BlockSpec((2, rows, wide), lambda i: (0, 0, i))
     up = pl.BlockSpec((width, cols), lambda i: (0, i))
     dwd = dwd.reshape(lead + (width,))
-    outs = [((rows, width), BF16), ((take, 3 * width), F32), ((take, width), F32), ((take, hidden), F32),
-            ((take * (hidden // width), width), F32), ((1, total), F32)]
+    outs = [((rows, width), BF16), ((take, 3 * width), F32), ((take, width), F32), ((take, part), F32),
+            ((take * part // width, width), F32), ((1, total), F32)]
     row_vec = pltpu.VMEM((1, width), F32)
     nsem = (len(chunks) + 3, npeer)
     return pl.pallas_call(
@@ -782,11 +862,11 @@
         in_specs=[full, vec, vec, whole(norm_t.shape), up, whole(ang.shape), tok, kvs, kvs, full, full,
                   whole(dwd.shape), whole(partw.shape), whole(partr.shape), vec, whole(dbe.shape)],
         out_specs=tuple(whole(s) for s, _ in outs),
-        scratch_shapes=halving_scratch(bits, parts, take, chunks, True) + [
+        scratch_shapes=halving_scratch(bits, parts, take, chunks, [1] * len(chunks)) + [
             pltpu.VMEM((3, rows, PAIR), F32), pltpu.VMEM((rows, width), F32),
             pltpu.VMEM(lead + (3 * width,), BF16), pltpu.VMEM((1, 3 * width), F32),
             row_vec, row_vec, row_vec, row_vec,
-            pltpu.VMEM((parts - 1, take, hidden), BF16), pltpu.VMEM((parts - 1, take, hidden), BF16),
+            pltpu.VMEM((parts - 1, take, part), BF16), pltpu.VMEM((parts - 1, take, part), BF16),
             pltpu.VMEM((bits + 1, 1, total), F32), pltpu.VMEM((npeer, 1, total), F32),
             pltpu.SemaphoreType.DMA(nsem), pltpu.SemaphoreType.DMA(nsem),
         ],
@@ -797,31 +877,35 @@
     )(x, gain, gain2, norm_t, w, ang, dq, dkv, dkvn, og, sg, dwd, partw, partr, dog, dbe)
 
 
-def finish_kernel(sizes, index_ref, ig_ref, dw_ref, dwd_ref, dwe_ref, dwr_ref, vec_ref,
+def finish_kernel(sizes, index_ref, ig_ref, dw_ref, dwd_ref, dwe0_ref, dwe1_ref, dwr0_ref, dwr1_ref, vec_ref,
                   ig_out, dw_out, dwd_out, dwe_out, dwr_out, *outs):
-    for src, dst in ((ig_ref, ig_out), (dw_ref, dw_out), (dwd_ref, dwd_out), (dwe_ref, dwe_out),
-                     (dwr_ref, dwr_out)):
+    for src, dst in ((ig_ref, ig_out), (dw_ref, dw_out), (dwd_ref, dwd_out)):
         dst[...] = src[...]
-
-    @pl.when(pl.program_id(0) == 0)
-    def _():
-        at = 0
-        for size, out in zip(sizes, outs):
-            own = out.shape[1]
-            row = jnp.broadcast_to(vec_ref[:, at:at + size], (8, size))
-            out[...] = pltpu.roll(row, lax.rem(size - index_ref[0] * own, size), 1)[:1, :own]
-            at += size
-
-
-def finish(index, ndev, sizes, ig, dw, dwd, dwe, dwr, vec):
-    mats = (ig, dw, dwd, dwe, dwr)
+    half = dwe0_ref.shape[1]
+    dwe_out[:, :half] = dwe0_ref[...]
+    dwe_out[:, half:] = dwe1_ref[...]
+    half = dwr0_ref.shape[0]
+    dwr_out[:half, :] = dwr0_ref[...]
+    dwr_out[half:, :] = dwr1_ref[...]
+    at = 0
+    for size, out in zip(sizes, outs):
+        own = out.shape[1]
+        row = jnp.broadcast_to(vec_ref[:, at:at + size], (8, size))
+        out[...] = pltpu.roll(row, lax.rem(size - index_ref[0] * own, size), 1)[:1, :own]
+        at += size
+
+
+def finish(index, ndev, sizes, ig, dw, dwd, dwe0, dwe1, dwr0, dwr1, vec):
+    mats = (ig, dw, dwd, dwe0, dwe1, dwr0, dwr1)
+    outs = [(m.shape, m.dtype) for m in (ig, dw, dwd)] + [
+        ((dwe0.shape[0], 2 * dwe0.shape[1]), F32), ((2 * dwr0.shape[0], dwr0.shape[1]), F32)]
+    outs += [((1, n // ndev), F32) for n in sizes]
     return pl.pallas_call(
         partial(finish_kernel, sizes),
-        out_shape=tuple(jax.ShapeDtypeStruct(m.shape, m.dtype) for m in mats)
-        + tuple(jax.ShapeDtypeStruct((1, n // ndev), F32) for n in sizes),
+        out_shape=tuple(jax.ShapeDtypeStruct(s, d) for s, d in outs),
         grid=(1,),
         in_specs=[pl.BlockSpec(memory_space=pltpu.SMEM)] + [whole(m.shape) for m in mats] + [whole(vec.shape)],
-        out_specs=tuple([whole(m.shape) for m in mats] + [whole((1, n // ndev)) for n in sizes]),
+        out_specs=tuple(whole(s) for s, _ in outs),
         compiler_params=params(),
         name="finish",
     )(index, *mats, vec)
@@ -864,14 +948,14 @@
     batch_parts = lax.axis_size("batch")
     ndev = batch_parts * seq_parts
     bits = batch_parts.bit_length() - 1
-    q, kv, do, n1t, n2, n2t = project(
+    q, kv, kvh, do, n1t, n2, n2t = project(
         tokens, ag, ash, mg, msh, qkv_weight, row(qkv_bias), ang, out_grad, dense_weight)
-    kvp = lax.ppermute(kv, "seq", onward)
+    kvp = lax.ppermute(kvh, "seq", onward)
     mid, slope, dwr, dog = mlp_fwd(
         ndev, n2, expand_weight, row(expand_bias), reduce_weight, out_grad)
     sg, dwe, dbe = mlp_back(n2t, expand_weight, reduce_weight, out_grad, slope)
 
-    o, dq, dkv, dkvn, partw, partr = attend(bits, seq_parts, flag, q, kv, kvp, do, dwe, dwr)
+    o, dq, dkv, dkvn, partw, partr, totw, totr = attend(bits, seq_parts, flag, q, kv, kvp, do, dwe, dwr)
     layer_out, dwd = dense(o, dense_weight, row(dense_bias), row(reduce_bias), mid, tokens, out_grad)
     input_grad, dw, dwd, dwe, dwr, vsum = tail(
         bits, seq_parts, tokens, ag, mg, n1t, qkv_weight, ang, dq, dkv, dkvn, out_grad, sg, dwd,
@@ -879,7 +963,7 @@
     index = lax.axis_index("batch") * seq_parts + place
     sizes = (width, width, 3 * width, width, width, width, dbe.shape[1])
     input_grad, dw, dwd, dwe, dwr, *vectors = finish(
-        index.astype(jnp.int32).reshape(1), ndev, sizes, input_grad, dw, dwd, dwe, dwr, vsum)
+        index.astype(jnp.int32).reshape(1), ndev, sizes, input_grad, dw, dwd, totw, dwe, totr, dwr, vsum)
     dag, das, dqb, dog, dmg, dms, dbe = [v.reshape(-1) for v in vectors]
     return (
         layer_out,

time: 388 us -> 371 us (0.956)
  Pallas kernels: 371 us -> 355 us
    pallas_call x1, Pallas kernels: 47.9 us -> 34 us  [mlp_back(): pl.pallas_call(mlp_back_kernel, grid=(hidden // FB,), out_shape=(jax.Shap...]
    pallas_call x1, Pallas kernels: 85.8 us -> 76.8 us  [tail(): pl.pallas_call(partial(tail_kernel, bits, parts, chunks), grid=(nstep,),...]
    pallas_call x1, Pallas kernels: 152 us -> 159 us  [attend(): pl.pallas_call(partial(attend_kernel, bits, parts, chunks, ends), grid=(s...]
  transfers between devices with their start and end apart: 1 -> 1, of which waited for: 0 -> 0; matrix products, arithmetic and copies ran while one was open for 0% -> 0% of each run, Pallas kernels for 25% -> 23%
where the time goes in v3:
time: 371 us; the launch traced here: 367 us
  Pallas kernels  355 us (96%)
  starting transfers between devices  6.41 us (2%)
    pallas_call x1, Pallas kernels, attend(): pl.pallas_call(partial(attend_kernel, bits, parts, chunks, ends), grid=(s...  159 us
    pallas_call x1, Pallas kernels, tail(): pl.pallas_call(partial(tail_kernel, bits, parts, chunks), grid=(nstep,),...  76.8 us
    pallas_call x1, Pallas kernels, mlp_fwd(): pl.pallas_call(partial(mlp_fwd_kernel, out_rows // ndev), grid=(hidden //...  49.2 us
    pallas_call x1, Pallas kernels, mlp_back(): pl.pallas_call(mlp_back_kernel, grid=(hidden // FB,), out_shape=(jax.Shap...  34 us
    pallas_call x1, Pallas kernels, project(): pl.pallas_call(project_kernel, grid=(width // wide,), out_shape=(jax.Shap...  21.7 us
    pallas_call x1, Pallas kernels, dense(): pl.pallas_call(dense_kernel, grid=(width // blk,), out_shape=(jax.ShapeDt...  10.7 us
  transfers between devices with their start and end apart: 1, of which 0 were waited for; matrix products, arithmetic and copies ran while one was open for 0% of the time, Pallas kernels for 23%

profile of v3, /device:TPU:0, one launch (start us, length us, event | category | flops | bytes accessed | tf_op | source)
XLA Modules:
  0.0 367.2 jit_solution(5065325094013609262)
XLA Ops:
  0.7 0.8 reduce-window.9
  1.5 1.3 fusion
  3.5 0.2 multiply_cosine_fusion
  3.7 0.6 pad_maximum_fusion.ang_ref
  4.3 21.7 %project.1 = (bf16[1024,1024]{1,0:T(8,128)(2,1)}, bf16[2,1024,1024]{2,1,0:T(8,128)(2,1)}, bf16[2,1024,512]{2,1,0:T(8,128)(2,1)}, bf16[1024,1024]{1,0:T(8,128)(2,...) custom-call(bf16[1024,1024]{1,0:T(8,128)(2,1)} %x_ref.5, ...), custom_call_target="tpu_custom_call" | custom-call | flops 8589934592 | bytes 25165824 | tf_op jit(solution)/shard_map/project/pallas_call | solution.py:160
  26.0 6.4 %collective-permute-start = (bf16[2,1024,512]{2,1,0:T(8,128)(2,1)}, bf16[2,1024,512]{2,1,0:T(8,128)(2,1)}, u32[]{:S(2)}, u32[]{:S(2)}) collective-permute-start(bf16[2,1024,512]{2,1,0:T(8,128)(2,1)} %get-tuple-element.58), channel_id=1, source_target_pairs={{0,1},{1,2},{2,3},{4,5},{5,6},{6,7},{8,9},{9,10},{10,11},{12,13},{... | collective-permute-start | bytes 6291464 | tf_op jit(solution)/shard_map/ppermute | solution.py:953
  32.4 49.2 %mlp_fwd.1 = (f32[1024,1024]{1,0:T(8,128)}, bf16[1024,4096]{1,0:T(8,128)(2,1)}, bf16[1024,4096]{1,0:T(8,128)(2,1)}, f32[1,1024]{1,0:T(1,128)}) custom-call(bf16[1024,1024]{1,0:T(8,128)(2,1)} %get-tuple-element.61.norm, bf16[1024,4096]{1,0:T(8,128)(2,1)} %we_ref.3, f32[1,4096]{1,0:T(1,128)} %bitcast.28, bf16[4096,1024]{1,0:T(8,128)(2,1)} %wr_ref.3, ...), custom_call_target="tpu_custom_call" | custom-call | flops 25769803776 | bytes 33554432 | tf_op jit(solution)/shard_map/mlp_fwd/pallas_call | solution.py:257
  81.7 34.0 %mlp_back.1 = (f32[1024,1024]{1,0:T(8,128)}, bf16[1024,4096]{1,0:T(8,128)(2,1)}, f32[1,4096]{1,0:T(1,128)}) custom-call(bf16[1024,1024]{1,0:T(8,128)(2,1)} %get-tuple-element.60.norm_t, bf16[1024,4096]{1,0:T(8,128)(2,1)} %we_ref.3, bf16[4096,1024]{1,0:T(8,128)(2,1)} %wr_ref.3, bf16[1024,1024]{1,0:T(8,128)(2,1)} %og_ref.9, ...), custom_call_target="tpu_custom_call" | custom-call | flops 25769803776 | bytes 33554432 | tf_op jit(solution)/shard_map/mlp_back/pallas_call | solution.py:274
  115.7 0.0 collective-permute-done.kvp_hbm
  115.7 158.7 %attend.1 = (bf16[1024,1024]{1,0:T(8,128)(2,1)}, bf16[1024,1024]{1,0:T(8,128)(2,1)}, bf16[2,1024,1024]{2,1,0:T(8,128)(2,1)}, bf16[2,1024,1024]{2,1,0:T(8,128)(2,...) custom-call(s32[1]{0:T(128)} %bitcast.3.flag_ref, ...), custom_call_target="tpu_custom_call" | custom-call | flops 64424509440 | bytes 20971520 | tf_op jit(solution)/shard_map/attend/pallas_call | solution.py:635
  274.3 10.7 %dense.1 = (bf16[1024,1024]{1,0:T(8,128)(2,1)}, bf16[1024,1024]{1,0:T(8,128)(2,1)}) custom-call(bf16[1024,1024]{1,0:T(8,128)(2,1)} %get-tuple-element.65.o_ref, bf16[1024,1024]{1,0:T(8,128)(2,1)} %wd_ref.3, f32[1,1024]{1,0:T(1,128)} %bitcast.32, f32[1,1024]{1,0:T(1,128)} %bitcast.33, f32[1024,1024]{1,0:T(8,128)} %get-tuple-element.66.mid_ref, ...), custom_call_target="tpu_custom_call" | custom-call | flops 4294967296 | bytes 12582912 | tf_op jit(solution)/shard_map/dense/pallas_call | solution.py:683
  285.1 76.8 %tail.1 = (bf16[1024,1024]{1,0:T(8,128)(2,1)}, f32[32,3072]{1,0:T(8,128)}, f32[32,1024]{1,0:T(8,128)}, f32[32,2048]{1,0:T(8,128)}, f32[64,1024]{1,0:T(8,128)}, /*index=5*/f32[1,12288]{1,0:T(1,128)}) custom-call(bf16[1024,1024]{1,0:T(8,128)(2,1)} %x_ref.5, f32[1,1024]{1,0:T(1,128)} %bitcast.35, f32[1,1024]{1,0:T(1,128)} %bitcast.37, ...), custom_call_target="tpu_custom_call" | custom-call | flops 12884901888 | bytes 8388608 | tf_op jit(solution)/shard_map/tail/pallas_call | solution.py:858
  361.9 4.0 %finish.1 = (bf16[1024,1024]{1,0:T(8,128)(2,1)}, f32[32,3072]{1,0:T(8,128)}, f32[32,1024]{1,0:T(8,128)}, f32[32,4096]{1,0:T(8,128)}, f32[128,1024]{1,0:T(8,128)}...) custom-call(s32[1]{0:T(128)} %bitcast.14.index_ref, ...), custom_call_target="tpu_custom_call" | custom-call | tf_op jit(solution)/shard_map/finish/pallas_call | solution.py:903
  365.9 1.2 copy.30
  (2 shorter events, 0.0 us)
Async XLA Ops:
  26.0 89.6 %collective-permute-start = (bf16[2,1024,512]{2,1,0:T(8,128)(2,1)}, bf16[2,1024,512]{2,1,0:T(8,128)(2,1)}, u32[]{:S(2)}, u32[]{:S(2)}) collective-permute-start(bf16[2,1024,512]{2,1,0:T(8,128)(2,1)} %get-tuple-element.58), channel_id=1, source_target_pairs={{0,1},{1,2},{2,3},{4,5},{5,6},{6,7},{8,9},{9,10},{10,11},{12,13},{... | collective-permute-start | bytes 6291464 | tf_op jit(solution)/shard_map/ppermute | solution.py:953
